TPU v7x, 256 devices: a whole 4x4x8 slice. The times are simulated.
256 devices in a mesh: dp: 32 (over z, y), tp: 8 (over x, core).
Axes of the slice: x: 4, y: 4, z: 8, core: 2. Of those that a mesh axis runs over, the one named last changes fastest.
Arguments:
- tokens: bfloat16 [3072, 2880], P('dp', 'tp'), may hold values from -100 to 100
- attn_gain: float32 [2880], replicated, may hold values from 0.1 to 1.9
- w_query: bfloat16 [2880, 2048], P(None, 'tp'), may hold values from -0.109375 to 0.109375
- w_keyvalue: bfloat16 [2880, 8, 128], P(None, 'tp'), may hold values from -0.109375 to 0.109375
- attn_sinks: float32 [32], P('tp'), may hold values from 2 to 6
- w_out: bfloat16 [2048, 2880], P('tp'), may hold values from -0.125 to 0.125
- window_cache: bfloat16 [3072, 8, 128, 128], P('dp', 'tp'), may hold values from -1000 to 1000
- positions: int32 [3072], P('dp'), may hold values from 0 to 511
- moe_gain: float32 [2880], replicated, may hold values from 0.1 to 1.9
- router: bfloat16 [2880, 32], P('tp'), may hold values from -0.109375 to 0.109375
- gate_up: bfloat16 [32, 2880, 2, 2880], P('dp', None, None, 'tp'), may hold values from -0.109375 to 0.109375
- w_down: bfloat16 [32, 2880, 2880], P('dp', None, 'tp'), may hold values from -0.109375 to 0.109375
- expert_ids: int32 [3072, 4], P('dp'), may hold values from 0 to 31, all different within a row; in each aligned block of 96 rows (0 to 95, 96 to 191, ...) at most 32 rows name the same one
Outputs:
- layer_out: float32 [3072, 2880], P('dp', 'tp')
Inputs may be any that keep to these rules, and one draw needn't show every extreme that they name: `expert_ids`: each row names 4 different experts. Within the rows of one index of dp no expert is named by more than 32 rows, a bound that some of these blocks reach.
All inputs are finite; a program needn't handle non-finite values.
Results may differ from a plain program's by a relative error of at most 0.0066.
Values may be sent and summed in bfloat16 or wider, within the bound.
A program may use at most 128 MiB of HBM per device.

v0:
```python
import jax
import jax.numpy as jnp
from jax import lax
from jax.experimental import pallas as pl
from jax.experimental.pallas import tpu as pltpu
from jax.sharding import PartitionSpec as P

norm_eps = 1e-05
rope_base = 150000.0
glu_alpha = 1.702


def sent_to_all(array, axis):
    copies = jnp.broadcast_to(array, (lax.axis_size(axis), *array.shape))
    return lax.all_to_all(copies, axis, split_axis=0, concat_axis=0, tiled=True)


def taken_together(array, axis):
    everything = sent_to_all(array, axis)
    return jnp.sum(everything, axis=0)


def laid_out(parts, dim):
    parts = jnp.moveaxis(parts, 0, dim)
    shape = parts.shape
    return parts.reshape(*shape[:dim], shape[dim] * shape[dim + 1], *shape[dim + 2 :])


def gathered_copies(array, axis, dim):
    return laid_out(sent_to_all(array, axis), dim)


def in_blocks(array, dim, peers):
    shape = array.shape
    parts = array.reshape(*shape[:dim], peers, shape[dim] // peers, *shape[dim + 1 :])
    return jnp.moveaxis(parts, dim, 0)


def sum_at_owner(array, axis, dim):
    peers = lax.axis_size(axis)
    parts = lax.all_to_all(in_blocks(array, dim, peers), axis, 0, 0, tiled=True)
    return jnp.sum(parts.astype(jnp.float32), axis=0)


def rope_tables(positions, head_size):
    half_size = head_size // 2
    exponent = jnp.arange(half_size, dtype=jnp.float32) * (2.0 / head_size)
    inverse = jnp.power(jnp.float32(rope_base), -exponent)
    angles = positions.astype(jnp.float32)[:, None] * inverse[None, :]
    return (jnp.cos(angles), jnp.sin(angles))


def rotate(values, cosine, sine_table):
    half_size = values.shape[-1] // 2
    first_half = values[..., :half_size]
    second_half = values[..., half_size:]
    return jnp.concatenate(
        [
            first_half * cosine - second_half * sine_table,
            second_half * cosine + first_half * sine_table,
        ],
        axis=-1,
    )


PAD = 384
NZ = 8
NY = 4
NX = 4
SLOTS = 32
CHUNK = NY * SLOTS
WIDE = 2 * NX * PAD
MESH = pl.DeviceIdType.MESH


def z_offset(j):
    return jnp.where(lax.rem(j, 2) == 1, lax.div(j + 1, 2), NZ - lax.div(j, 2))


def experts_body(
    hid, placer, chi, clo, resid, wgu_hbm, wdn_hbm, out,
    rows, acts, wgu, wdn, placed, made, back,
    wsem, lsem, d_send, d_recv, r_send, r_recv, x_send, x_recv,
):
    dp = lax.axis_index("dp")
    tp = lax.axis_index("tp")
    z, y = lax.div(dp, NY), lax.rem(dp, NY)
    xx, core = lax.div(tp, 2), lax.rem(tp, 2)
    right = lax.rem(xx + 1, NX) * 2 + core
    left = lax.rem(xx + NX - 1, NX) * 2 + core
    across = lax.rem(xx + 2, NX) * 2 + core
    sib = xx * 2 + (1 - core)

    def flip(t):
        return t + 1 - 2 * core

    def cols(t):
        return pl.ds(pl.multiple_of(t * PAD, PAD), PAD)

    get_gu = pltpu.make_async_copy(wgu_hbm, wgu, wsem.at[0])
    get_dn = pltpu.make_async_copy(wdn_hbm, wdn, wsem.at[1])
    get_gu.start()
    get_dn.start()

    barrier = pltpu.get_barrier_semaphore()

    def greet(i, c):
        pl.semaphore_signal(
            barrier, inc=1, device_id=(lax.rem(dp + i, NZ * NY), tp), device_id_type=MESH
        )
        return c

    lax.fori_loop(1, NZ * NY, greet, 0)
    for t in (right, left, sib):
        pl.semaphore_signal(barrier, inc=1, device_id=(dp, t), device_id_type=MESH)
    pl.semaphore_wait(barrier, NZ * NY - 1 + 3)

    def dispatch_copy(j, i):
        dz = lax.rem(z + NZ - z_offset(j) , NZ)
        dest = lax.rem(dz + NZ, NZ) * NY + lax.rem(y + NY - i, NY)
        return pltpu.make_async_remote_copy(
            src_ref=placed.at[pl.ds(pl.multiple_of(dest * SLOTS, SLOTS), SLOTS), :],
            dst_ref=rows.at[j, pl.ds(pl.multiple_of(i * SLOTS, SLOTS), SLOTS), cols(tp)],
            send_sem=d_send.at[j * NY + i],
            recv_sem=d_recv.at[j * NY + i],
            device_id=(dest, tp),
            device_id_type=MESH,
        )

    own_in = pltpu.make_async_copy(
        placed.at[pl.ds(pl.multiple_of(dp * SLOTS, SLOTS), SLOTS), :],
        rows.at[0, pl.ds(0, SLOTS), cols(tp)],
        lsem.at[0],
    )

    def dispatch(j, c):
        zd = lax.rem(z + NZ - z_offset(j), NZ)
        part = pl.ds(pl.multiple_of(zd * CHUNK, CHUNK), CHUNK)
        placed[part, :] = jnp.dot(
            placer[part, :], hid[...], preferred_element_type=jnp.float32
        ).astype(jnp.bfloat16)

        @pl.when(j == 0)
        def _():
            own_in.start()

        @pl.when(j > 0)
        def _():
            dispatch_copy(j, 0).start()

        for i in range(1, NY):
            dispatch_copy(j, i).start()
        return c

    lax.fori_loop(0, NZ, dispatch, 0)

    def xcopy(buf, ph, kind, j, part, col, dest):
        ref = buf.at[j, part, cols(col)]
        return pltpu.make_async_remote_copy(
            src_ref=ref,
            dst_ref=ref,
            send_sem=x_send.at[ph, kind, j],
            recv_sem=x_recv.at[ph, kind, j],
            device_id=(dp, dest),
            device_id_type=MESH,
        )

    allr = pl.ds(0, CHUNK)
    top = pl.ds(0, CHUNK // 2)
    bot = pl.ds(CHUNK // 2, CHUNK // 2)

    def send_own(buf, ph, j):
        xcopy(buf, ph, 0, j, allr, tp, right).start()
        xcopy(buf, ph, 1, j, allr, tp, left).start()
        xcopy(buf, ph, 2, j, allr, tp, sib).start()

    def send_on(buf, ph, j):
        xcopy(buf, ph, 0, j, allr, left, right).wait_recv()
        xcopy(buf, ph, 3, j, top, left, right).start()
        xcopy(buf, ph, 4, j, allr, left, sib).start()
        xcopy(buf, ph, 1, j, allr, right, left).wait_recv()
        xcopy(buf, ph, 5, j, bot, right, left).start()
        xcopy(buf, ph, 6, j, allr, right, sib).start()

    def send_far(buf, ph, j):
        xcopy(buf, ph, 3, j, top, across, right).wait_recv()
        xcopy(buf, ph, 5, j, bot, across, left).wait_recv()
        xcopy(buf, ph, 7, j, allr, across, sib).start()

    def all_in(buf, ph, j):
        xcopy(buf, ph, 2, j, allr, sib, sib).wait_recv()
        xcopy(buf, ph, 4, j, allr, flip(left), sib).wait_recv()
        xcopy(buf, ph, 6, j, allr, flip(right), sib).wait_recv()
        xcopy(buf, ph, 7, j, allr, flip(across), sib).wait_recv()

    def back_copy(j, i):
        home = lax.rem(z + z_offset(j), NZ) * NY + lax.rem(y + i, NY)
        return pltpu.make_async_remote_copy(
            src_ref=made.at[j, pl.ds(pl.multiple_of(i * SLOTS, SLOTS), SLOTS), :],
            dst_ref=back.at[pl.ds(pl.multiple_of(dp * SLOTS, SLOTS), SLOTS), :],
            send_sem=r_send.at[j * NY + i],
            recv_sem=r_recv.at[dp],
            device_id=(home, tp),
            device_id_type=MESH,
        )

    own_back = pltpu.make_async_copy(
        made.at[0, pl.ds(0, SLOTS), :],
        back.at[pl.ds(pl.multiple_of(dp * SLOTS, SLOTS), SLOTS), :],
        lsem.at[1],
    )

    def step(t, c):
        @pl.when(t < NZ)
        def _():
            @pl.when(t == 0)
            def _():
                own_in.wait()

            @pl.when(t > 0)
            def _():
                dispatch_copy(t, 0).wait_recv()

            for i in range(1, NY):
                dispatch_copy(t, i).wait_recv()
            send_own(rows, 0, t)

        @pl.when((t >= 1) & (t < NZ + 1))
        def _():
            send_on(rows, 0, t - 1)

        @pl.when((t >= 2) & (t < NZ + 2))
        def _():
            send_far(rows, 0, t - 2)

        @pl.when(t == 3)
        def _():
            get_gu.wait()

        @pl.when((t >= 3) & (t < NZ + 3))
        def _():
            j = t - 3
            all_in(rows, 0, j)
            mixed = jnp.dot(rows[j], wgu[...], preferred_element_type=jnp.float32)
            gate = mixed[:, :PAD]
            up = mixed[:, PAD:]
            act = gate * jax.nn.sigmoid(glu_alpha * gate) * (up + 1.0)
            acts[j, :, cols(tp)] = act.astype(jnp.bfloat16)
            send_own(acts, 1, j)

        @pl.when((t >= 4) & (t < NZ + 4))
        def _():
            send_on(acts, 1, t - 4)

        @pl.when((t >= 5) & (t < NZ + 5))
        def _():
            send_far(acts, 1, t - 5)

        @pl.when(t == 6)
        def _():
            get_dn.wait()

        @pl.when(t >= 6)
        def _():
            j = t - 6
            all_in(acts, 1, j)
            made[j] = jnp.dot(acts[j], wdn[...], preferred_element_type=jnp.float32).astype(
                jnp.bfloat16
            )

            @pl.when(j == 0)
            def _():
                own_back.start()

            @pl.when(j > 0)
            def _():
                back_copy(j, 0).start()

            for i in range(1, NY):
                back_copy(j, i).start()

        return c

    lax.fori_loop(0, NZ + 6, step, 0)

    def await_back(i, c):
        peer = lax.rem(dp + i, NZ * NY)
        pltpu.make_async_remote_copy(
            src_ref=made.at[0, pl.ds(0, SLOTS), :],
            dst_ref=back.at[pl.ds(pl.multiple_of(peer * SLOTS, SLOTS), SLOTS), :],
            send_sem=r_send.at[1],
            recv_sem=r_recv.at[peer],
            device_id=(peer, tp),
            device_id_type=MESH,
        ).wait_recv()
        return c

    own_back.wait()
    lax.fori_loop(1, NZ * NY, await_back, 0)
    got = back[...]
    total = jnp.dot(chi[...], got, preferred_element_type=jnp.float32) + jnp.dot(
        clo[...], got, preferred_element_type=jnp.float32
    )
    out[...] = resid[...] + total[:, : out.shape[1]]

    def sent(n, c):
        dispatch_copy(lax.div(n, NY), lax.rem(n, NY)).wait_send()
        back_copy(lax.div(n, NY), lax.rem(n, NY)).wait_send()
        return c

    lax.fori_loop(1, NZ * NY, sent, 0)

    def sent_x(j, c):
        for ph, buf in ((0, rows), (1, acts)):
            for kind in range(8):
                part = top if kind == 3 else bot if kind == 5 else allr
                xcopy(buf, ph, kind, j, part, tp, right).wait_send()
        return c

    lax.fori_loop(0, NZ, sent_x, 0)


def experts_kernel(hid, placer, chi, clo, resid, wgu, wdn):
    vmem = pl.BlockSpec(memory_space=pltpu.VMEM)
    hbm = pl.BlockSpec(memory_space=pl.ANY)
    dma = pltpu.SemaphoreType.DMA
    bf = jnp.bfloat16
    return pl.pallas_call(
        experts_body,
        out_shape=jax.ShapeDtypeStruct(resid.shape, jnp.float32),
        in_specs=[vmem] * 5 + [hbm] * 2,
        out_specs=vmem,
        scratch_shapes=[
            pltpu.VMEM((NZ, CHUNK, WIDE), bf),
            pltpu.VMEM((NZ, CHUNK, WIDE), bf),
            pltpu.VMEM((WIDE, 2 * PAD), bf),
            pltpu.VMEM((WIDE, PAD), bf),
            pltpu.VMEM((NZ * CHUNK, PAD), bf),
            pltpu.VMEM((NZ, CHUNK, PAD), bf),
            pltpu.VMEM((NZ * CHUNK, PAD), bf),
            dma((2,)),
            dma((2,)),
            dma((NZ * NY,)),
            dma((NZ * NY,)),
            dma((NZ * NY,)),
            dma((NZ * NY,)),
            dma((2, 8, NZ)),
            dma((2, 8, NZ)),
        ],
        compiler_params=pltpu.CompilerParams(
            collective_id=0, has_side_effects=True, vmem_limit_bytes=48 * 1024 * 1024
        ),
        name="experts",
    )(hid, placer, chi, clo, resid, wgu, wdn)


def on_device(
    tokens,
    attn_gain,
    w_query,
    w_keyvalue,
    attn_sinks,
    w_out,
    window_cache,
    positions,
    moe_gain,
    router,
    gate_up,
    w_down,
    expert_ids,
):
    tp_count = lax.axis_size("tp")
    dp_count = lax.axis_size("dp")
    seq_count, col_count = tokens.shape
    full_width = col_count * tp_count
    col_start = lax.axis_index("tp") * col_count
    head_size = w_keyvalue.shape[2] // 2
    kv_local = w_keyvalue.shape[1]
    q_local = w_query.shape[1] // head_size
    group_size = q_local // kv_local
    window = window_cache.shape[2]
    attn_slice = lax.dynamic_slice_in_dim(attn_gain, col_start, col_count)
    moe_slice = lax.dynamic_slice_in_dim(moe_gain, col_start, col_count)
    tok_wide = tokens.astype(jnp.float32)
    attn_sq = taken_together(jnp.sum(tok_wide * tok_wide, axis=1), "tp")
    normed = (
        tok_wide * lax.rsqrt(attn_sq / full_width + norm_eps)[:, None] * attn_slice[None, :]
    ).astype(jnp.bfloat16)
    kv_flat = w_keyvalue.reshape(full_width, kv_local * 2 * head_size)
    piece_rows = gathered_copies(normed, "tp", 1)
    queries = jnp.dot(piece_rows, w_query, preferred_element_type=jnp.float32)
    fresh_rows = jnp.dot(piece_rows, kv_flat, preferred_element_type=jnp.float32)
    cosine, sine_table = rope_tables(positions, head_size)
    rot_queries = rotate(
        queries.reshape(seq_count, q_local, head_size), cosine[:, None, :], sine_table[:, None, :]
    ).astype(jnp.bfloat16)
    fresh_rows = fresh_rows.reshape(seq_count, kv_local, 2 * head_size)
    new_key = rotate(fresh_rows[..., :head_size], cosine[:, None, :], sine_table[:, None, :])
    new_entry = jnp.concatenate([new_key, fresh_rows[..., head_size:]], axis=-1).astype(
        jnp.bfloat16
    )
    slot_ids = jnp.arange(window, dtype=jnp.int32)
    is_current = slot_ids[None, :] == (positions % window)[:, None]
    cache_now = jnp.where(is_current[:, None, :, None], new_entry[:, :, None, :], window_cache)
    is_valid = (positions[:, None] - slot_ids[None, :]) % window <= positions[:, None]
    grouped = rot_queries.reshape(seq_count, kv_local, group_size, head_size)
    scores = jnp.einsum(
        "skgh,skwh->skgw", grouped, cache_now[..., :head_size], preferred_element_type=jnp.float32
    ) * head_size ** (-0.5)
    scores = jnp.where(is_valid[:, None, None, :], scores, -jnp.inf)
    sink_col = attn_sinks.reshape(kv_local, group_size)[None, :, :, None]
    peak_score = jnp.maximum(jnp.max(scores, axis=-1, keepdims=True), sink_col)
    raised = jnp.exp(scores - peak_score)
    denominator = jnp.sum(raised, axis=-1, keepdims=True) + jnp.exp(sink_col - peak_score)
    prob_bf = (raised / denominator).astype(jnp.bfloat16)
    attended = jnp.einsum(
        "skgw,skwh->skgh", prob_bf, cache_now[..., head_size:], preferred_element_type=jnp.float32
    ).astype(jnp.bfloat16)
    partial_out = jnp.dot(
        attended.reshape(seq_count, q_local * head_size), w_out, preferred_element_type=jnp.float32
    )
    residual = tok_wide + sum_at_owner(partial_out.astype(jnp.bfloat16), "tp", 1)
    experts = router.shape[1]
    top_count = expert_ids.shape[1]
    local_experts = gate_up.shape[0]
    ff_local = gate_up.shape[3]
    capacity = min(seq_count, max(2, 8 * seq_count * top_count // (3 * experts)))
    moe_sq = jnp.sum(residual * residual, axis=1)
    router_wide = router.astype(jnp.float32)
    total_sq = taken_together(moe_sq, "tp")
    moe_scale = lax.rsqrt(total_sq / full_width + norm_eps)[:, None]
    scaled = residual * moe_scale * moe_slice[None, :]
    logits = taken_together(jnp.dot(scaled, router_wide, precision=lax.Precision.HIGHEST), "tp")
    hidden_rows = scaled.astype(jnp.bfloat16)
    expert_iota = jnp.arange(experts, dtype=jnp.int32)
    chosen = expert_ids[:, :, None] == expert_iota[None, None, :]
    picked = jnp.sum(jnp.where(chosen, logits[:, None, :], 0.0), axis=-1)
    raised_logits = jnp.exp(picked)
    route_weights = raised_logits / jnp.sum(raised_logits, axis=1, keepdims=True)
    assign = expert_ids.reshape(-1)
    onehot = (assign[:, None] == expert_iota[None, :]).astype(jnp.int32)
    earlier = jnp.cumsum(onehot, axis=0) - onehot
    slot_of = jnp.sum(earlier * onehot, axis=1)
    target = (assign * capacity + slot_of).reshape(seq_count, top_count)
    spot_ids = jnp.arange(experts * capacity, dtype=jnp.int32)
    slot_hits = target[:, :, None] == spot_ids[None, None, :]
    placer = jnp.transpose(jnp.any(slot_hits, axis=1)).astype(jnp.bfloat16)
    combiner = jnp.sum(jnp.where(slot_hits, route_weights[:, :, None], 0.0), axis=1)
    comb_hi = combiner.astype(jnp.bfloat16)
    comb_lo = (combiner - comb_hi.astype(jnp.float32)).astype(jnp.bfloat16)
    hidden_pad = jnp.pad(hidden_rows, ((0, 0), (0, PAD - col_count)))
    wgu = jnp.pad(
        gate_up.reshape(tp_count, col_count, 2, ff_local),
        ((0, 0), (0, PAD - col_count), (0, 0), (0, PAD - ff_local)),
    ).reshape(tp_count * PAD, 2 * PAD)
    wdn = jnp.pad(
        w_down.reshape(tp_count, ff_local, col_count),
        ((0, 0), (0, PAD - ff_local), (0, PAD - col_count)),
    ).reshape(tp_count * PAD, PAD)
    return experts_kernel(hidden_pad, placer, comb_hi, comb_lo, residual, wgu, wdn)


def solution(mesh):
    in_specs = (
        P("dp", "tp"),
        P(),
        P(None, "tp"),
        P(None, "tp", None),
        P("tp"),
        P("tp", None),
        P("dp", "tp", None, None),
        P("dp"),
        P(),
        P("tp", None),
        P("dp", None, None, "tp"),
        P("dp", None, "tp"),
        P("dp", None),
    )
    out_specs = P("dp", "tp")
    return jax.shard_map(
        on_device, mesh=mesh, in_specs=in_specs, out_specs=out_specs, check_vma=False
    )
```

profile of v0, /device:TPU:1, one launch (start us, length us, event | category | flops | bytes accessed | tf_op | source)
XLA Modules:
  0.0 200.5 jit_solution(11533910334496343572)
XLA Ops:
  0.0 1.1 fusion.8
  1.1 0.6 broadcast_in_dim.57
  1.7 6.4 %all-to-all-start = ((f32[8,1,96]{2,1,0:T(1,128)}), f32[8,1,96]{2,1,0:T(1,128)S(1)}, u32[]{:S(2)}, u32[]{:S(2)}) async-start(f32[8,1,96]{2,1,0:T(1,128)} %broadcast_in_dim.57), calls=%async_computation | async-start | bytes 8192 | tf_op jit(solution)/shard_map/all_to_all | solution.py:15
  8.1 1.3 fusion.26
  9.5 0.7 fusion.38
  10.2 0.8 dynamic_slice.6
  11.0 1.7 all-to-all-done
  12.7 1.0 fusion.10
  13.7 0.9 broadcast_in_dim.58
  14.6 4.8 %all-to-all-start.1 = ((bf16[8,96,360]{2,1,0:T(8,128)(2,1)}), bf16[8,96,360]{2,1,0:T(8,128)(2,1)}, u32[]{:S(2)}, u32[]{:S(2)}) async-start(bf16[8,96,360]{2,1,0:T(8,128)(2,1)} %broadcast_in_dim.58), calls=%async_computation.1 | async-start | bytes 1179648 | tf_op jit(solution)/shard_map/all_to_all | solution.py:15
  19.3 4.6 %copy.99 = bf16[96,1,128,128]{2,3,0,1:T(8,128)(2,1)} copy(bf16[96,1,128,128]{3,2,1,0:T(8,128)(2,1)} %param.19) | data formatting | bytes 6291456 | tf_op args[6]
  24.0 1.8 copy.98
  26.1 0.7 iota_compare_fusion.4
  26.7 0.7 multiply_cosine_fusion.1
  27.5 2.0 %all-to-all-done.1 = bf16[8,96,360]{2,1,0:T(8,128)(2,1)} async-done(((bf16[8,96,360]{2,1,0:T(8,128)(2,1)}), bf16[8,96,360]{2,1,0:T(8,128)(2,1)}, u32[]{:S(2)}, u32[]{:S(2)}) %all-to-all-start.1) | async-done | bytes 552992 | tf_op jit(solution)/shard_map/all_to_all | solution.py:15
  29.5 2.1 %copy.97 = bf16[96,8,360]{2,1,0:T(8,128)(2,1)} copy(bf16[96,8,360]{2,0,1:T(8,128)(2,1)} %bitcast.1) | data formatting | bytes 1105920 | tf_op jit(solution)/shard_map/transpose | solution.py:24
  31.6 1.7 reshape.375
  33.2 1.4 convolution_bitcast_fusion
  34.7 1.6 fusion.36
  36.2 0.7 fusion.34
  36.9 1.7 reshape.387
  38.6 0.6 fusion.40
  39.5 0.9 pad_maximum_fusion.1
  40.4 3.8 %broadcast_select_fusion = bf16[96,1,128,128]{2,3,0,1:T(8,128)(2,1)S(1)} fusion(bf16[96,1,128,128]{2,3,0,1:T(8,128)(2,1)} %copy.99, pred[96,128]{1,0:T(8,128)(4,1)} %iota_compare_fusion.4, bf16[96,128]{1,0:T(8,128)(2,1)S(1)} %pad_maximum_fusion.1), kind=kLoop, calls=%fused_computation.1 | loop fusion | flops 1572864 | bytes 6328320 | tf_op jit(solution)/shard_map/jit(_where)/select_n | solution.py:404
  44.2 0.6 fusion.39
  44.8 0.3 fusion.7
  45.2 1.0 fusion.5
  46.3 0.6 convolution_convert_fusion
  46.9 0.8 reshape.381
  47.7 0.9 copy.117
  48.6 4.4 %all-to-all-start.2 = ((bf16[8,96,360]{2,1,0:T(8,128)(2,1)}), bf16[8,96,360]{2,1,0:T(8,128)(2,1)S(1)}, u32[]{:S(2)}, u32[]{:S(2)}) async-start(bf16[8,96,360]{2,1,0:T(8,128)(2,1)} %bitcast.67), calls=%async_computation.2 | async-start | bytes 1179648 | tf_op jit(solution)/shard_map/all_to_all | solution.py:41
  53.1 0.9 reduce-window.6
  54.6 8.5 %all-to-all-done.2 = bf16[8,96,360]{2,1,0:T(8,128)(2,1)S(1)} async-done(((bf16[8,96,360]{2,1,0:T(8,128)(2,1)}), bf16[8,96,360]{2,1,0:T(8,128)(2,1)S(1)}, u32[]{:S(2)}, u32[]{:S(2)}) %all-to-all-start.2) | async-done | bytes 552992 | tf_op jit(solution)/shard_map/all_to_all | solution.py:41
  63.3 0.6 broadcast_in_dim.62
  63.9 4.2 %all-to-all-start.3 = ((f32[8,1,96]{2,1,0:T(1,128)}), f32[8,1,96]{2,1,0:T(1,128)S(1)}, u32[]{:S(2)}, u32[]{:S(2)}) async-start(f32[8,1,96]{2,1,0:T(1,128)} %broadcast_in_dim.62), calls=%async_computation.3 | async-start | bytes 8192 | tf_op jit(solution)/shard_map/all_to_all | solution.py:15
  68.1 0.3 fusion.2
  68.4 0.8 dynamic_slice.7
  69.4 12.4 %copy.111 = bf16[1,2880,2,360]{3,2,1,0:T(2,128)(2,1)} copy(bf16[1,2880,2,360]{1,3,2,0:T(8,128)(2,1)} %param.23) | data formatting | bytes 8294400 | tf_op jit(solution)/shard_map/reshape | solution.py:453
  81.8 8.3 %pad.13 = bf16[8,384,2,384]{3,2,1,0:T(2,128)(2,1)} pad(bf16[8,360,2,360]{3,2,1,0:T(2,128)(2,1)} %bitcast.73, bf16[]{:T(256)} %constant.55.clone.1), padding=0_0x0_24x0_0x0_24 | pad | bytes 8865794 | tf_op jit(solution)/shard_map/jit(_pad)/pad | solution.py:452
  90.1 5.3 %copy.114 = bf16[384,8,2,384]{3,1,2,0:T(8,128)(2,1)} copy(bf16[384,8,2,384]{3,2,1,0:T(2,128)(2,1)} %bitcast.72) | data formatting | bytes 9437184
  95.4 4.1 %copy.112 = bf16[1,2880,360]{2,1,0:T(8,128)(2,1)} copy(bf16[1,2880,360]{1,2,0:T(8,128)(2,1)} %param.24) | data formatting | bytes 4147200 | tf_op jit(solution)/shard_map/reshape | solution.py:457
  99.5 3.3 %pad.14 = bf16[8,384,384]{2,1,0:T(8,128)(2,1)} pad(bf16[8,360,360]{2,1,0:T(8,128)(2,1)} %bitcast.74, bf16[]{:T(256)} %constant.55.clone.1), padding=0_0x0_24x0_24 | pad | bytes 4432898 | tf_op jit(solution)/shard_map/jit(_pad)/pad | solution.py:456
  103.2 0.7 broadcast_in_dim.98
  103.8 4.8 %all-to-all-start.4 = ((f32[8,96,32]{1,2,0:T(8,128)}), f32[8,96,32]{1,2,0:T(8,128)S(1)}, u32[]{:S(2)}, u32[]{:S(2)}) async-start(f32[8,96,32]{1,2,0:T(8,128)} %broadcast_in_dim.98), calls=%async_computation.4 | async-start | bytes 262144 | tf_op jit(solution)/shard_map/all_to_all | solution.py:15
  108.8 5.1 %all-to-all-done.4 = f32[8,96,32]{1,2,0:T(8,128)S(1)} async-done(((f32[8,96,32]{1,2,0:T(8,128)}), f32[8,96,32]{1,2,0:T(8,128)S(1)}, u32[]{:S(2)}, u32[]{:S(2)}) %all-to-all-start.4) | async-done | bytes 98336 | tf_op jit(solution)/shard_map/all_to_all | solution.py:15
  114.3 1.7 copy-done.1
  116.0 83.8 %experts.1 = f32[96,360]{1,0:T(8,128)S(1)} custom-call(bf16[96,384]{1,0:T(8,128)(2,1)S(1)} %pad.12.hid, bf16[1024,96]{1,0:T(8,128)(2,1)S(1)} %bitcast.70, bf16[96,1024]{1,0:T(8,128)(2,1)S(1)} %get-tuple-element.6.chi, bf16[96,1024]{1,0:T(8,128)(2,1)S(1)} %get-tuple-element.5.clo, f32[96,360]{1,0:T(8,128)S(1)} %get-tuple-element.8.resid, ...), custom_call_target="tpu_custom_call" | custom-call | tf_op jit(solution)/shard_map/experts/pallas_call | solution.py:328
  199.8 0.7 copy.119
  (60 shorter events, 2.6 us)
Async XLA Ops:
  0.0 46.3 %copy-start = (bf16[256,2880]{0,1:T(8,128)(2,1)S(1)}, bf16[256,2880]{0,1:T(8,128)(2,1)}, u32[]{:S(2)}) copy-start(bf16[256,2880]{0,1:T(8,128)(2,1)} %param.18) | copy-start | bytes 4423684
  1.7 11.0 %all-to-all-start = ((f32[8,1,96]{2,1,0:T(1,128)}), f32[8,1,96]{2,1,0:T(1,128)S(1)}, u32[]{:S(2)}, u32[]{:S(2)}) async-start(f32[8,1,96]{2,1,0:T(1,128)} %broadcast_in_dim.57), calls=%async_computation | async-start | bytes 8192 | tf_op jit(solution)/shard_map/all_to_all | solution.py:15
  10.2 16.5 %copy-start.11 = (f32[96]{0:T(128)}, f32[96]{0:T(128)S(1)}, u32[]{:S(2)}) copy-start(f32[96]{0:T(128)S(1)} %get-tuple-element.15) | copy-start | bytes 1156
  14.6 15.0 %all-to-all-start.1 = ((bf16[8,96,360]{2,1,0:T(8,128)(2,1)}), bf16[8,96,360]{2,1,0:T(8,128)(2,1)}, u32[]{:S(2)}, u32[]{:S(2)}) async-start(bf16[8,96,360]{2,1,0:T(8,128)(2,1)} %broadcast_in_dim.58), calls=%async_computation.1 | async-start | bytes 1179648 | tf_op jit(solution)/shard_map/all_to_all | solution.py:15
  19.3 7.4 %copy-start.12 = (f32[32]{0:T(128)}, f32[32]{0:T(128)S(1)}, u32[]{:S(2)}) copy-start(f32[32]{0:T(128)S(1)} %negate_power_fusion) | copy-start | bytes 388
  24.0 1.8 copy-start.8
  25.9 3.6 %copy-start.3 = (s32[96,4]{1,0:T(8,128)}, s32[96,4]{1,0:T(8,128)S(1)}, u32[]{:S(2)}) copy-start(s32[96,4]{1,0:T(8,128)S(1)} %copy.104) | copy-start | bytes 4612
  38.6 0.7 copy-start.5
  38.6 0.7 copy-start.6
  40.4 3.8 %copy-start.9 = (pred[96,128]{1,0:T(8,128)(4,1)S(1)}, pred[96,128]{1,0:T(8,128)(4,1)}, u32[]{:S(2)}) copy-start(pred[96,128]{1,0:T(8,128)(4,1)} %fusion.26) | copy-start | bytes 36868
  44.2 0.7 copy-start.10
  46.9 6.1 %copy-start.4 = (s32[96,4]{1,0:T(8,128)S(1)}, s32[96,4]{1,0:T(8,128)}, u32[]{:S(2)}) copy-start(s32[96,4]{1,0:T(8,128)} %copy-done.3) | copy-start | bytes 4612
  47.7 15.5 %copy-start.2 = (bf16[96,360]{1,0:T(8,128)(2,1)S(1)}, bf16[96,360]{1,0:T(8,128)(2,1)}, u32[]{:S(2)}) copy-start(bf16[96,360]{1,0:T(8,128)(2,1)} %param.13) | copy-start | bytes 207364
  48.6 14.5 %all-to-all-start.2 = ((bf16[8,96,360]{2,1,0:T(8,128)(2,1)}), bf16[8,96,360]{2,1,0:T(8,128)(2,1)S(1)}, u32[]{:S(2)}, u32[]{:S(2)}) async-start(bf16[8,96,360]{2,1,0:T(8,128)(2,1)} %bitcast.67), calls=%async_computation.2 | async-start | bytes 1179648 | tf_op jit(solution)/shard_map/all_to_all | solution.py:41
  63.9 38.9 %all-to-all-start.3 = ((f32[8,1,96]{2,1,0:T(1,128)}), f32[8,1,96]{2,1,0:T(1,128)S(1)}, u32[]{:S(2)}, u32[]{:S(2)}) async-start(f32[8,1,96]{2,1,0:T(1,128)} %broadcast_in_dim.62), calls=%async_computation.3 | async-start | bytes 8192 | tf_op jit(solution)/shard_map/all_to_all | solution.py:15
  99.5 3.4 %copy-start.7 = (bf16[360,32]{0,1:T(8,128)(2,1)S(1)}, bf16[360,32]{0,1:T(8,128)(2,1)}, u32[]{:S(2)}) copy-start(bf16[360,32]{0,1:T(8,128)(2,1)} %param.22) | copy-start | bytes 69124
  103.8 10.1 %all-to-all-start.4 = ((f32[8,96,32]{1,2,0:T(8,128)}), f32[8,96,32]{1,2,0:T(8,128)S(1)}, u32[]{:S(2)}, u32[]{:S(2)}) async-start(f32[8,96,32]{1,2,0:T(8,128)} %broadcast_in_dim.98), calls=%async_computation.4 | async-start | bytes 262144 | tf_op jit(solution)/shard_map/all_to_all | solution.py:15
  114.3 1.7 copy-start.1
where the time goes:
time: 202 us; the launch traced here: 200 us
  Pallas kernels  83.8 us (41%)
  local copies, waits for them, and re-layouts  55.6 us (28%)
  starting transfers between devices  24.6 us (12%)
  waiting for transfers between devices  17.4 us (9%)
  other arithmetic  14.3 us (7%)
  matrix products  4.43 us (2%)
    pallas_call x1, Pallas kernels, experts_kernel(): pl.pallas_call(experts_body, out_shape=jax.ShapeDtypeStruct(resid.shape,...  83.8 us
    all_to_all x4, starting transfers between devices, sent_to_all(): return lax.all_to_all(copies, axis, split_axis=0, concat_axis=0, tiled=True)  20.2 us
    unnamed x31, local copies, waits for them, and re-layouts  14.4 us
    reshape x1, local copies, waits for them, and re-layouts, on_device(): gate_up.reshape(tp_count, col_count, 2, ff_local)  12.4 us
    all_to_all x4, waiting for transfers between devices, sent_to_all(): return lax.all_to_all(copies, axis, split_axis=0, concat_axis=0, tiled=True)  8.84 us
    all_to_all x1, waiting for transfers between devices, sum_at_owner(): parts = lax.all_to_all(in_blocks(array, dim, peers), axis, 0, 0, tiled=True)  8.52 us
    pad x1, local copies, waits for them, and re-layouts, on_device(): jnp.pad(gate_up.reshape(tp_count, col_count, 2, ff_local), ((0, 0), (0, P...  8.28 us
    all_to_all x1, starting transfers between devices, sum_at_owner(): parts = lax.all_to_all(in_blocks(array, dim, peers), axis, 0, 0, tiled=True)  4.4 us
  transfers between devices with their start and end apart: 5, of which 4 were waited for; matrix products, arithmetic and copies ran while one was open for 24% of the time, Pallas kernels for 0%

commit v1 on v0

v1 whole, which is shorter than its diff:
```python
import math

import jax
import jax.numpy as jnp
from jax import lax
from jax.experimental import pallas as pl
from jax.experimental.pallas import tpu as pltpu
from jax.sharding import PartitionSpec as P

norm_eps = 1e-05
rope_base = 150000.0
glu_alpha = 1.702

COL = 360
PAD = 384
FULL = 2880
NZ = 8
NY = 4
NX = 4
NTP = 2 * NX
SLOTS = 32
CHUNK = NY * SLOTS
WIDE = NTP * PAD
TOK = 96
HEADS = 4
HD = 64
LANES = 128
SPAN = 8 * TOK
MESH = pl.DeviceIdType.MESH
NT = (((1,), (1,)), ((), ()))
F32 = jnp.float32
BF = jnp.bfloat16


def z_offset(j):
    return jnp.where(lax.rem(j, 2) == 1, lax.div(j + 1, 2), NZ - lax.div(j, 2))


def dot_nt(a, b):
    return lax.dot_general(a, b, NT, preferred_element_type=F32)


def split3(v):
    hi = v.astype(BF)
    rest = v - hi.astype(F32)
    mid = rest.astype(BF)
    low = (rest - mid.astype(F32)).astype(BF)
    return hi, mid, low


def spread_blocks(src, dst, rows, row_step):
    def part(n, c):
        at = pl.ds(pl.multiple_of(n * row_step, row_step), row_step)
        for b in range(NTP):
            low = b * COL // LANES * LANES
            off = b * COL - low
            high = min(low + 4 * LANES, FULL)
            piece = src[at, low:high]
            dst[at, b * PAD + 2 * LANES : (b + 1) * PAD] = jnp.zeros((row_step, LANES), dst.dtype)
            dst[at, b * PAD : b * PAD + COL] = piece[:, off : off + COL]
        return c

    lax.fori_loop(0, rows // row_step, part, 0)


def layer_body(
    tokens, again, mgain, sinks, pos, router_t, ids_t,
    wq_hbm, wkv_hbm, wo_hbm, cache_hbm, gu_hbm, dn_hbm,
    out,
    rows, acts, wgu, wdn, placed, made, back,
    toks, wq, wkv, wo, cache, raw_gu, raw_dn,
    gain_pad, own_gain, tok_pad, qbuf, kvb, scb, resid, hid, placer, comb_hi, comb_lo,
    mine_f, mine_b, sib_b, chip_b, recv_b, table, small, small_t,
    wsem, lsem, d_send, d_recv, r_send, r_recv, x_send, x_recv,
    o_send, o_recv, a_send, a_recv,
):
    dp = lax.axis_index("dp")
    tp = lax.axis_index("tp")
    z, y = lax.div(dp, NY), lax.rem(dp, NY)
    xx, core = lax.div(tp, 2), lax.rem(tp, 2)
    right = lax.rem(xx + 1, NX) * 2 + core
    left = lax.rem(xx + NX - 1, NX) * 2 + core
    across = lax.rem(xx + 2, NX) * 2 + core
    sib = xx * 2 + (1 - core)

    def flip(t):
        return t + 1 - 2 * core

    def cols(t):
        return pl.ds(pl.multiple_of(t * PAD, PAD), PAD)

    barrier = pltpu.get_barrier_semaphore()

    def greet(i, c):
        pl.semaphore_signal(
            barrier, inc=1, device_id=(lax.rem(dp + i, NZ * NY), tp), device_id_type=MESH
        )
        return c

    def greet_tp(i, c):
        pl.semaphore_signal(
            barrier, inc=1, device_id=(dp, lax.rem(tp + i, NTP)), device_id_type=MESH
        )
        return c

    lax.fori_loop(1, NTP, greet_tp, 0)
    lax.fori_loop(1, NZ * NY, greet, 0)

    get_q = [
        pltpu.make_async_copy(
            wq_hbm.at[pl.ds(b * COL, COL), :], wq.at[pl.ds(b * PAD, COL), :], wsem.at[b]
        )
        for b in range(NTP)
    ]
    get_kv = [
        pltpu.make_async_copy(
            wkv_hbm.at[pl.ds(b * COL, COL), :], wkv.at[pl.ds(b * PAD, COL), :], wsem.at[8 + b]
        )
        for b in range(NTP)
    ]
    get_o = [
        pltpu.make_async_copy(
            wo_hbm.at[pl.ds(b * COL, COL), :], wo.at[pl.ds(b * PAD, COL), :], wsem.at[16 + b]
        )
        for b in range(NTP)
    ]
    get_cache = pltpu.make_async_copy(cache_hbm, cache, wsem.at[24])
    get_gu = [
        pltpu.make_async_copy(gu_hbm.at[u], raw_gu.at[pl.ds(u * PAD, COL), :], wsem.at[25 + u])
        for u in range(2)
    ]
    get_dn = pltpu.make_async_copy(dn_hbm, raw_dn.at[pl.ds(0, COL), :], wsem.at[27])
    for group in (get_gu, [get_dn], get_q, get_kv, [get_cache], get_o):
        for get in group:
            get.start()

    tok_pad[...] = jnp.zeros((TOK, PAD), F32)
    tok_pad[:, :COL] = tokens[...].astype(F32)
    toks[0, :, cols(tp)] = tok_pad[...].astype(BF)

    def xcopy(buf, ph, kind, j, part, col, dest):
        ref = buf.at[j, part, cols(col)]
        return pltpu.make_async_remote_copy(
            src_ref=ref,
            dst_ref=ref,
            send_sem=x_send.at[ph, kind, j],
            recv_sem=x_recv.at[ph, kind, j],
            device_id=(dp, dest),
            device_id_type=MESH,
        )

    def parts_of(buf):
        n = buf.shape[1]
        return pl.ds(0, n), pl.ds(0, n // 2), pl.ds(n // 2, n // 2)

    def send_own(buf, ph, j):
        allr, top, bot = parts_of(buf)
        xcopy(buf, ph, 0, j, allr, tp, right).start()
        xcopy(buf, ph, 1, j, allr, tp, left).start()
        xcopy(buf, ph, 2, j, allr, tp, sib).start()

    def send_on(buf, ph, j):
        allr, top, bot = parts_of(buf)
        xcopy(buf, ph, 0, j, allr, left, right).wait_recv()
        xcopy(buf, ph, 3, j, top, left, right).start()
        xcopy(buf, ph, 4, j, allr, left, sib).start()
        xcopy(buf, ph, 1, j, allr, right, left).wait_recv()
        xcopy(buf, ph, 5, j, bot, right, left).start()
        xcopy(buf, ph, 6, j, allr, right, sib).start()

    def send_far(buf, ph, j):
        allr, top, bot = parts_of(buf)
        xcopy(buf, ph, 3, j, top, across, right).wait_recv()
        xcopy(buf, ph, 5, j, bot, across, left).wait_recv()
        xcopy(buf, ph, 7, j, allr, across, sib).start()

    def all_in(buf, ph, j):
        allr, top, bot = parts_of(buf)
        xcopy(buf, ph, 2, j, allr, sib, sib).wait_recv()
        xcopy(buf, ph, 4, j, allr, flip(left), sib).wait_recv()
        xcopy(buf, ph, 6, j, allr, flip(right), sib).wait_recv()
        xcopy(buf, ph, 7, j, allr, flip(across), sib).wait_recv()

    def all_sent(buf, ph, j):
        allr, top, bot = parts_of(buf)
        for kind in range(8):
            part = top if kind == 3 else bot if kind == 5 else allr
            xcopy(buf, ph, kind, j, part, tp, right).wait_send()

    pl.semaphore_wait(barrier, NZ * NY - 1 + NTP - 1)
    send_own(toks, 2, 0)

    for b in range(NTP):
        gain_pad[:, b * PAD + 2 * LANES : (b + 1) * PAD] = jnp.zeros((1, LANES), F32)
        gain_pad[:, b * PAD : b * PAD + COL] = again[:, b * COL : (b + 1) * COL]
        own = mgain[:, b * COL : (b + 1) * COL]

        @pl.when(tp == b)
        def _():
            own_gain[...] = jnp.zeros((1, PAD), F32)
            own_gain[:, :COL] = own

    small[...] = jnp.zeros((8, LANES), F32)
    small[0:1, :TOK] = pos[...].astype(F32)
    pos_col = jnp.transpose(jnp.broadcast_to(small[0:1, :], (LANES, LANES)))[:TOK]
    lane = lax.broadcasted_iota(jnp.int32, (TOK, LANES), 1)
    inverse = jnp.exp(
        lax.rem(lane, HD // 2).astype(F32) * (-2.0 / HD * math.log(rope_base))
    )
    angles = pos_col * inverse
    first = lax.rem(lane, HD) < HD // 2
    table[0] = jnp.cos(angles)
    sine = jnp.sin(angles)
    table[1] = jnp.where(first, -sine, sine)
    table[2] = pos_col

    experts = NZ * NY
    e_iota = lax.broadcasted_iota(jnp.int32, (experts, TOK), 0)
    named = e_iota == ids_t[0:1, :]
    for k in range(1, ids_t.shape[0]):
        named = named | (e_iota == ids_t[k : k + 1, :])
    before = (
        lax.broadcasted_iota(jnp.int32, (TOK, TOK), 0)
        < lax.broadcasted_iota(jnp.int32, (TOK, TOK), 1)
    ).astype(F32)
    named_f = named.astype(F32)
    slot = jnp.dot(named_f, before, preferred_element_type=F32)
    slot = jnp.where(named, slot, -1.0)
    s_iota = lax.broadcasted_iota(jnp.int32, (SLOTS, TOK), 0).astype(F32)
    for e in range(experts):
        placer[e * SLOTS : (e + 1) * SLOTS, :] = (
            s_iota == slot[e : e + 1, :]
        ).astype(F32)

    send_on(toks, 2, 0)
    for u, get in enumerate(get_gu):
        get.wait()
    raw_gu[COL:PAD, :] = jnp.zeros((PAD - COL, FULL), BF)
    raw_gu[PAD + COL : 2 * PAD, :] = jnp.zeros((PAD - COL, FULL), BF)
    spread_blocks(raw_gu, wgu, 2 * PAD, 48)
    send_far(toks, 2, 0)
    get_dn.wait()
    raw_dn[COL:PAD, :] = jnp.zeros((PAD - COL, FULL), BF)
    spread_blocks(raw_dn, wdn, PAD, 48)
    for group, ref in ((get_q, wq), (get_kv, wkv), (get_o, wo)):
        for b, get in enumerate(group):
            get.wait()
            ref[b * PAD + COL : (b + 1) * PAD, :] = jnp.zeros((PAD - COL, ref.shape[1]), BF)
    all_in(toks, 2, 0)

    wide = toks[0].astype(F32)
    mean = jnp.sum(wide * wide, axis=1, keepdims=True) * (1.0 / FULL)
    normed = (wide * lax.rsqrt(mean + norm_eps) * gain_pad[...]).astype(BF)
    queries = jnp.dot(normed, wq[...], preferred_element_type=F32)
    fresh = jnp.dot(normed, wkv[...], preferred_element_type=F32)

    def turned(v):
        swapped = jnp.where(
            first, pltpu.roll(v, LANES - HD // 2, axis=1), pltpu.roll(v, HD // 2, axis=1)
        )
        return v * table[0] + swapped * table[1]

    entry = jnp.where(lane < HD, turned(fresh), fresh).astype(BF).astype(F32)
    qbuf[...] = jnp.zeros((SPAN, LANES), F32)
    kvb[...] = jnp.zeros((SPAN, LANES), F32)
    for g in range(HEADS):
        tile = g // 2
        if g % 2 == 0:
            rotated = turned(queries[:, tile * LANES : (tile + 1) * LANES]).astype(BF).astype(F32)
        head = rotated if g % 2 == 0 else pltpu.roll(rotated, HD, axis=1)
        qbuf[pl.ds(g, TOK, stride=8), :] = jnp.where(lane < HD, head * HD**-0.5, 0.0)
        kvb[pl.ds(g, TOK, stride=8), :] = entry
    get_cache.wait()

    def score(n, c):
        for u in range(8):
            s = n * 8 + u
            at = pl.ds(pl.multiple_of(s * 8, 8), 8)
            scb[at, :] = dot_nt(qbuf[at, :].astype(BF), cache[s])
        return c

    lax.fori_loop(0, TOK // 8, score, 0)
    sub = lax.broadcasted_iota(jnp.int32, (8, LANES), 0)
    sink = jnp.where(
        sub == 0,
        sinks[0],
        jnp.where(sub == 1, sinks[1], jnp.where(sub == 2, sinks[2], sinks[3])),
    )[:, :1]
    slots = lax.broadcasted_iota(jnp.int32, (8, LANES), 1)

    def soften(n, c):
        for u in range(8):
            s = n * 8 + u
            at = pl.ds(pl.multiple_of(s * 8, 8), 8)
            where_now = table[2, pl.ds(s, 1), :].astype(jnp.int32)
            current = slots == lax.rem(where_now, LANES)
            newest = jnp.sum(qbuf[at, :] * kvb[at, :], axis=1, keepdims=True)
            raw = jnp.where(current, newest, scb[at, :])
            raw = jnp.where(slots <= where_now, raw, -jnp.inf)
            peak = jnp.maximum(jnp.max(raw, axis=1, keepdims=True), sink)
            raised = jnp.exp(raw - peak)
            total = jnp.sum(raised, axis=1, keepdims=True) + jnp.exp(sink - peak)
            probs = (raised / total).astype(BF)
            newest_prob = (jnp.exp(newest - peak) / total).astype(BF).astype(F32)
            kept = jnp.where(current, 0.0, probs.astype(F32)).astype(BF)
            mixed = jnp.dot(kept, cache[s], preferred_element_type=F32)
            scb[at, :] = mixed + newest_prob * kvb[at, :]
        return c

    lax.fori_loop(0, TOK // 8, soften, 0)
    tiles = []
    for tile in range(2):
        even = scb[pl.ds(2 * tile, TOK, stride=8), :]
        odd = scb[pl.ds(2 * tile + 1, TOK, stride=8), :]
        tiles.append(jnp.where(lane < HD, pltpu.roll(even, HD, axis=1), odd).astype(BF))
    attended = jnp.concatenate(tiles, axis=1)

    def out_block(owner):
        return dot_nt(attended, wo[cols(owner), :])

    for n in range(NX):
        mine_b[n] = out_block(2 * n + 1 - core).astype(BF)
    to_sib = pltpu.make_async_remote_copy(
        src_ref=mine_b,
        dst_ref=sib_b,
        send_sem=o_send.at[0],
        recv_sem=o_recv.at[0],
        device_id=(dp, sib),
        device_id_type=MESH,
    )
    to_sib.start()
    for n in range(NX):
        mine_f[n] = out_block(2 * n + core)
    to_sib.wait_recv()

    def to_chip(i):
        owner = lax.rem(xx + i, NX)
        return pltpu.make_async_remote_copy(
            src_ref=chip_b.at[owner],
            dst_ref=recv_b.at[i],
            send_sem=o_send.at[i],
            recv_sem=o_recv.at[i],
            device_id=(dp, owner * 2 + core),
            device_id_type=MESH,
        )

    for i in (2, 1, 3):
        owner = lax.rem(xx + i, NX)
        chip_b[owner] = (mine_f[owner] + sib_b[owner].astype(F32)).astype(BF)
        to_chip(i).start()
    total = tok_pad[...] + (mine_f[xx] + sib_b[xx].astype(F32))
    for i in (1, 3, 2):
        to_chip(i).wait_recv()
    for i in (1, 2, 3):
        total = total + recv_b[i].astype(F32)
    resid[...] = total

    lifted = total * own_gain[...]
    wide_rows = jnp.zeros((LANES - TOK, PAD), BF)
    logit_part = jnp.zeros((experts, LANES), F32)
    for piece in split3(lifted):
        logit_part = logit_part + dot_nt(router_t[...], jnp.concatenate([piece, wide_rows], axis=0))
    square_part = jnp.zeros((8, LANES), F32)
    ones = jnp.ones((8, PAD), BF)
    for piece in split3(total * total):
        square_part = square_part + dot_nt(ones, jnp.concatenate([piece, wide_rows], axis=0))
    small_t[tp, 0:experts, :] = logit_part
    small_t[tp, experts : experts + 8, :] = square_part

    def share(i):
        return pltpu.make_async_remote_copy(
            src_ref=small_t.at[tp],
            dst_ref=small_t.at[tp],
            send_sem=a_send.at[i],
            recv_sem=a_recv.at[i],
            device_id=(dp, lax.rem(tp + i, NTP)),
            device_id_type=MESH,
        )

    for i in range(1, NTP):
        share(i).start()
    for i in range(1, NTP):
        share(i).wait_recv()
    summed = small_t[0]
    for n in range(1, NTP):
        summed = summed + small_t[n]
    scale_row = lax.rsqrt(summed[experts : experts + 1, :] * (1.0 / FULL) + norm_eps)
    scale_col = jnp.transpose(jnp.broadcast_to(scale_row, (LANES, LANES)))[:TOK, :1]
    hid[...] = (resid[...] * scale_col * own_gain[...]).astype(BF)

    def dispatch_copy(j, i):
        dest = lax.rem(z + NZ + NZ - z_offset(j), NZ) * NY + lax.rem(y + NY - i, NY)
        return pltpu.make_async_remote_copy(
            src_ref=placed.at[pl.ds(pl.multiple_of(dest * SLOTS, SLOTS), SLOTS), :],
            dst_ref=rows.at[j, pl.ds(pl.multiple_of(i * SLOTS, SLOTS), SLOTS), cols(tp)],
            send_sem=d_send.at[j * NY + i],
            recv_sem=d_recv.at[j * NY + i],
            device_id=(dest, tp),
            device_id_type=MESH,
        )

    own_in = pltpu.make_async_copy(
        placed.at[pl.ds(pl.multiple_of(dp * SLOTS, SLOTS), SLOTS), :],
        rows.at[0, pl.ds(0, SLOTS), cols(tp)],
        lsem.at[0],
    )

    def dispatch(j, c):
        zd = lax.rem(z + NZ + NZ - z_offset(j), NZ)
        part = pl.ds(pl.multiple_of(zd * CHUNK, CHUNK), CHUNK)
        placed[part, :] = jnp.dot(
            placer[part, :].astype(BF), hid[...], preferred_element_type=F32
        ).astype(BF)

        @pl.when(j == 0)
        def _():
            own_in.start()

        @pl.when(j > 0)
        def _():
            dispatch_copy(j, 0).start()

        for i in range(1, NY):
            dispatch_copy(j, i).start()
        return c

    lax.fori_loop(0, NZ, dispatch, 0)

    logits = summed[0:experts, :TOK] * scale_row[:, :TOK]
    lifted_logits = jnp.where(named, jnp.exp(logits), 0.0)
    weights = lifted_logits / jnp.sum(lifted_logits, axis=0, keepdims=True)
    for e in range(experts):
        at = slice(e * SLOTS, (e + 1) * SLOTS)
        placer[at, :] = placer[at, :] * weights[e : e + 1, :]
    for n in range(NZ):
        at = slice(n * CHUNK, (n + 1) * CHUNK)
        piece = jnp.transpose(placer[at, :])
        hi = piece.astype(BF)
        comb_hi[:, at] = hi
        comb_lo[:, at] = (piece - hi.astype(F32)).astype(BF)

    def back_copy(j, i):
        home = lax.rem(z + z_offset(j), NZ) * NY + lax.rem(y + i, NY)
        return pltpu.make_async_remote_copy(
            src_ref=made.at[j, pl.ds(pl.multiple_of(i * SLOTS, SLOTS), SLOTS), :],
            dst_ref=back.at[pl.ds(pl.multiple_of(dp * SLOTS, SLOTS), SLOTS), :],
            send_sem=r_send.at[j * NY + i],
            recv_sem=r_recv.at[dp],
            device_id=(home, tp),
            device_id_type=MESH,
        )

    own_back = pltpu.make_async_copy(
        made.at[0, pl.ds(0, SLOTS), :],
        back.at[pl.ds(pl.multiple_of(dp * SLOTS, SLOTS), SLOTS), :],
        lsem.at[1],
    )

    def step(t, c):
        @pl.when(t < NZ)
        def _():
            @pl.when(t == 0)
            def _():
                own_in.wait()

            @pl.when(t > 0)
            def _():
                dispatch_copy(t, 0).wait_recv()

            for i in range(1, NY):
                dispatch_copy(t, i).wait_recv()
            send_own(rows, 0, t)

        @pl.when((t >= 1) & (t < NZ + 1))
        def _():
            send_on(rows, 0, t - 1)

        @pl.when((t >= 2) & (t < NZ + 2))
        def _():
            send_far(rows, 0, t - 2)

        @pl.when((t >= 3) & (t < NZ + 3))
        def _():
            j = t - 3
            all_in(rows, 0, j)
            mixed = dot_nt(rows[j], wgu[...])
            gate = mixed[:, :PAD]
            up = mixed[:, PAD:]
            act = gate * jax.nn.sigmoid(glu_alpha * gate) * (up + 1.0)
            acts[j, :, cols(tp)] = act.astype(BF)
            send_own(acts, 1, j)

        @pl.when((t >= 4) & (t < NZ + 4))
        def _():
            send_on(acts, 1, t - 4)

        @pl.when((t >= 5) & (t < NZ + 5))
        def _():
            send_far(acts, 1, t - 5)

        @pl.when(t >= 6)
        def _():
            j = t - 6
            all_in(acts, 1, j)
            made[j] = dot_nt(acts[j], wdn[...]).astype(BF)

            @pl.when(j == 0)
            def _():
                own_back.start()

            @pl.when(j > 0)
            def _():
                back_copy(j, 0).start()

            for i in range(1, NY):
                back_copy(j, i).start()

        return c

    lax.fori_loop(0, NZ + 6, step, 0)

    def await_back(i, c):
        peer = lax.rem(dp + i, NZ * NY)
        pltpu.make_async_remote_copy(
            src_ref=made.at[0, pl.ds(0, SLOTS), :],
            dst_ref=back.at[pl.ds(pl.multiple_of(peer * SLOTS, SLOTS), SLOTS), :],
            send_sem=r_send.at[1],
            recv_sem=r_recv.at[peer],
            device_id=(peer, tp),
            device_id_type=MESH,
        ).wait_recv()
        return c

    own_back.wait()
    lax.fori_loop(1, NZ * NY, await_back, 0)
    got = back[...]
    answer = (
        resid[...]
        + jnp.dot(comb_hi[...], got, preferred_element_type=F32)
        + jnp.dot(comb_lo[...], got, preferred_element_type=F32)
    )
    out[...] = answer[:, :COL]

    to_sib.wait_send()
    for i in range(1, NX):
        to_chip(i).wait_send()
    for i in range(1, NTP):
        share(i).wait_send()
    all_sent(toks, 2, 0)

    def sent(n, c):
        dispatch_copy(lax.div(n, NY), lax.rem(n, NY)).wait_send()
        back_copy(lax.div(n, NY), lax.rem(n, NY)).wait_send()
        return c

    lax.fori_loop(1, NZ * NY, sent, 0)

    def sent_x(j, c):
        all_sent(rows, 0, j)
        all_sent(acts, 1, j)
        return c

    lax.fori_loop(0, NZ, sent_x, 0)


def on_device(
    tokens,
    attn_gain,
    w_query,
    w_keyvalue,
    attn_sinks,
    w_out,
    window_cache,
    positions,
    moe_gain,
    router,
    gate_up,
    w_down,
    expert_ids,
):
    vmem = pl.BlockSpec(memory_space=pltpu.VMEM)
    smem = pl.BlockSpec(memory_space=pltpu.SMEM)
    hbm = pl.BlockSpec(memory_space=pl.ANY)
    dma = pltpu.SemaphoreType.DMA
    vm = pltpu.VMEM
    router_t = jnp.pad(jnp.transpose(router), ((0, 0), (0, PAD - COL)))
    return pl.pallas_call(
        layer_body,
        out_shape=jax.ShapeDtypeStruct(tokens.shape, F32),
        in_specs=[vmem, vmem, vmem, smem, vmem, vmem, vmem] + [hbm] * 6,
        out_specs=vmem,
        scratch_shapes=[
            vm((NZ, CHUNK, WIDE), BF),
            vm((NZ, CHUNK, WIDE), BF),
            vm((2 * PAD, WIDE), BF),
            vm((PAD, WIDE), BF),
            vm((NZ * CHUNK, PAD), BF),
            vm((NZ, CHUNK, PAD), BF),
            vm((NZ * CHUNK, PAD), BF),
            vm((1, TOK, WIDE), BF),
            vm((WIDE, HEADS * HD), BF),
            vm((WIDE, 2 * HD), BF),
            vm((WIDE, HEADS * HD), BF),
            vm((TOK, LANES, 2 * HD), BF),
            vm((2 * PAD, FULL), BF),
            vm((PAD, FULL), BF),
            vm((1, WIDE), F32),
            vm((1, PAD), F32),
            vm((TOK, PAD), F32),
            vm((SPAN, LANES), F32),
            vm((SPAN, LANES), F32),
            vm((SPAN, LANES), F32),
            vm((TOK, PAD), F32),
            vm((TOK, PAD), BF),
            vm((NZ * CHUNK, TOK), F32),
            vm((TOK, NZ * CHUNK), BF),
            vm((TOK, NZ * CHUNK), BF),
            vm((NX, TOK, PAD), F32),
            vm((NX, TOK, PAD), BF),
            vm((NX, TOK, PAD), BF),
            vm((NX, TOK, PAD), BF),
            vm((NX, TOK, PAD), BF),
            vm((3, TOK, LANES), F32),
            vm((8, LANES), F32),
            vm((NTP, 40, LANES), F32),
            dma((28,)),
            dma((2,)),
            dma((NZ * NY,)),
            dma((NZ * NY,)),
            dma((NZ * NY,)),
            dma((NZ * NY,)),
            dma((3, 8, NZ)),
            dma((3, 8, NZ)),
            dma((NX,)),
            dma((NX,)),
            dma((NTP,)),
            dma((NTP,)),
        ],
        compiler_params=pltpu.CompilerParams(
            collective_id=0, has_side_effects=True, vmem_limit_bytes=60 * 1024 * 1024
        ),
        name="layer",
    )(
        tokens,
        attn_gain[None, :],
        moe_gain[None, :],
        attn_sinks,
        positions[None, :],
        router_t,
        jnp.transpose(expert_ids),
        w_query,
        w_keyvalue.reshape(FULL, 2 * HD),
        jnp.transpose(w_out),
        window_cache.reshape(TOK, LANES, 2 * HD),
        jnp.transpose(gate_up[0], (1, 2, 0)),
        jnp.transpose(w_down[0]),
    )


def solution(mesh):
    in_specs = (
        P("dp", "tp"),
        P(),
        P(None, "tp"),
        P(None, "tp", None),
        P("tp"),
        P("tp", None),
        P("dp", "tp", None, None),
        P("dp"),
        P(),
        P("tp", None),
        P("dp", None, None, "tp"),
        P("dp", None, "tp"),
        P("dp", None),
    )
    out_specs = P("dp", "tp")
    return jax.shard_map(
        on_device, mesh=mesh, in_specs=in_specs, out_specs=out_specs, check_vma=False
    )
```

time: 202 us -> 129 us (0.64)
  local copies, waits for them, and re-layouts: 55.6 us -> 5.55 us
  Pallas kernels: 83.8 us -> 123 us
  starting transfers between devices: 24.6 us -> 0 us
  waiting for transfers between devices: 17.4 us -> 0 us
  other arithmetic: 14.3 us -> 0 us
  matrix products: 4.43 us -> 0 us
    pallas_call x1, Pallas kernels: 83.8 us -> 123 us  [on_device(): pl.pallas_call(layer_body, out_shape=jax.ShapeDtypeStruct(tokens.shape, F...]
    all_to_all x5 -> x0, starting transfers between devices: 24.6 us -> none  [the longest x4 20.2 us: sent_to_all(): return lax.all_to_all(copies, axis, split_axis=0, concat_axis=0, tiled=True)]
    reshape x6 -> x0, local copies, waits for them, and re-layouts: 21.5 us -> none  [the longest x1 12.4 us: on_device(): gate_up.reshape(tp_count, col_count, 2, ff_local)]
    all_to_all x5 -> x0, waiting for transfers between devices: 17.4 us -> none  [the longest x4 8.84 us: sent_to_all(): return lax.all_to_all(copies, axis, split_axis=0, concat_axis=0, tiled=True)]
    unnamed x31 -> x1, local copies, waits for them, and re-layouts: 14.4 us -> 1.58 us
    pad x3 -> x1, local copies, waits for them, and re-layouts: 11.6 us -> 1.35 us  [on_device(): router_t = jnp.pad(jnp.transpose(router), ((0, 0), (0, PAD - COL)))]
    dot_general x6 -> x0, matrix products: 4.43 us -> none  [the longest x1 1.43 us: on_device(): jnp.dot(piece_rows, kv_flat, preferred_element_type=jnp.float32)]
    select_n x1 -> x0, other arithmetic: 3.8 us -> none  [on_device(): jnp.where(is_current[:, None, :, None], new_entry[:, :, None, :], window_...]
  transfers between devices with their start and end apart: 5 -> 0, of which waited for: 4 -> 0; matrix products, arithmetic and copies ran while one was open for 24% -> 0% of each run, Pallas kernels for 0% -> 0%
where the time goes in v1:
time: 129 us
  Pallas kernels  123 us (95%)
  local copies, waits for them, and re-layouts  5.55 us (4%)
    pallas_call x1, Pallas kernels, on_device(): pl.pallas_call(layer_body, out_shape=jax.ShapeDtypeStruct(tokens.shape, F...  123 us

profile of v1, /device:TPU:1, one launch (start us, length us, event | category | flops | bytes accessed | tf_op | source)
XLA Modules:
  0.0 129.0 jit_solution(9299854997007330027)
XLA Ops:
  0.0 1.3 %broadcast_in_dim.9.again = f32[1,2880]{1,0:T(1,128)} reshape(f32[2880]{0:T(1024)} %param.14) | data formatting | bytes 23040 | tf_op jit(solution)/shard_map/broadcast_in_dim | solution.py:645
  1.3 1.3 %broadcast_in_dim.10.mgain = f32[1,2880]{1,0:T(1,128)} reshape(f32[2880]{0:T(1024)} %param.21) | data formatting | bytes 23040 | tf_op jit(solution)/shard_map/broadcast_in_dim | solution.py:646
  2.6 1.4 %pad.4.router_t = bf16[32,384]{1,0:T(8,128)(2,1)} pad(bf16[32,360]{1,0:T(8,128)(2,1)} %bitcast.17, bf16[]{:T(256)} %constant.2.clone.1), padding=0_0x0_24 | pad | bytes 47618 | tf_op jit(solution)/shard_map/jit(_pad)/pad | solution.py:586
  4.0 123.4 %layer.1 = f32[96,360]{1,0:T(8,128)} custom-call(bf16[96,360]{1,0:T(8,128)(2,1)} %tokens.1, f32[1,2880]{1,0:T(1,128)} %broadcast_in_dim.9.again, f32[1,2880]{1,0:T(1,128)} %broadcast_in_dim.10.mgain, f32[4]{0:T(128)} %sinks.1, s32[1,96]{1,0:T(1,128)} %bitcast.19, bf16[32,384]{1,0:T(8,128)(2,1)} %pad.4.router_t, s32[4,96]{1,0:T(4,128)} %bitcast.18, ...), custom_call_target="tpu_custom_call" | custom-call | tf_op jit(solution)/shard_map/layer/pallas_call | solution.py:587
  127.4 1.6 %copy.15 = f32[96,360]{1,0:T(8,128)} copy(f32[96,360]{1,0:T(8,128)} %layer.1) | data formatting | bytes 276480

commit v2 on v1

--- a/solution.py
+++ b/solution.py
@@ -32,8 +32,19 @@
 BF = jnp.bfloat16
 
 
+ORDER = (0, 7, 2, 4, 5, 3, 6, 1)
+OWN = ORDER.index(0)
+AHEAD = 3
+STRAIGHT_ROWS = 1
+STRAIGHT_ACTS = 2
+STRAIGHT_TOKENS = True
+
+
 def z_offset(j):
-    return jnp.where(lax.rem(j, 2) == 1, lax.div(j + 1, 2), NZ - lax.div(j, 2))
+    offset = 0
+    for n, value in enumerate(ORDER):
+        offset = jnp.where(j == n, value, offset)
+    return offset
 
 
 def dot_nt(a, b):
@@ -64,15 +75,15 @@
 
 
 def layer_body(
-    tokens, again, mgain, sinks, pos, router_t, ids_t,
+    tokens, gains, sinks, pos, router_t, ids_t,
     wq_hbm, wkv_hbm, wo_hbm, cache_hbm, gu_hbm, dn_hbm,
     out,
     rows, acts, wgu, wdn, placed, made, back,
     toks, wq, wkv, wo, cache, raw_gu, raw_dn,
     gain_pad, own_gain, tok_pad, qbuf, kvb, scb, resid, hid, placer, comb_hi, comb_lo,
-    mine_f, mine_b, sib_b, chip_b, recv_b, table, small, small_t,
+    mine_f, mine_b, sib_b, chip_b, recv_b, table, small, small_t, posb, router_pad, scale_out, scale_in,
     wsem, lsem, d_send, d_recv, r_send, r_recv, x_send, x_recv,
-    o_send, o_recv, a_send, a_recv,
+    o_send, o_recv, a_send, a_recv, s_send, s_recv,
 ):
     dp = lax.axis_index("dp")
     tp = lax.axis_index("tp")
@@ -130,7 +141,7 @@
         for u in range(2)
     ]
     get_dn = pltpu.make_async_copy(dn_hbm, raw_dn.at[pl.ds(0, COL), :], wsem.at[27])
-    for group in (get_gu, [get_dn], get_q, get_kv, [get_cache], get_o):
+    for group in (get_q, get_kv, [get_cache], get_o, get_gu, [get_dn]):
         for get in group:
             get.start()
 
@@ -153,25 +164,52 @@
         n = buf.shape[1]
         return pl.ds(0, n), pl.ds(0, n // 2), pl.ds(n // 2, n // 2)
 
+    def straight(ph, j):
+        if ph == 2:
+            return STRAIGHT_TOKENS
+        return j < STRAIGHT_ROWS if ph == 0 else j >= NZ - STRAIGHT_ACTS
+
     def send_own(buf, ph, j):
         allr, top, bot = parts_of(buf)
+
+        @pl.when(straight(ph, j))
+        def _():
+            xcopy(buf, ph, 3, j, allr, tp, across).start()
+
         xcopy(buf, ph, 0, j, allr, tp, right).start()
         xcopy(buf, ph, 1, j, allr, tp, left).start()
         xcopy(buf, ph, 2, j, allr, tp, sib).start()
 
     def send_on(buf, ph, j):
         allr, top, bot = parts_of(buf)
+        relayed = jnp.logical_not(straight(ph, j))
         xcopy(buf, ph, 0, j, allr, left, right).wait_recv()
-        xcopy(buf, ph, 3, j, top, left, right).start()
+
+        @pl.when(relayed)
+        def _():
+            xcopy(buf, ph, 3, j, top, left, right).start()
+
         xcopy(buf, ph, 4, j, allr, left, sib).start()
         xcopy(buf, ph, 1, j, allr, right, left).wait_recv()
-        xcopy(buf, ph, 5, j, bot, right, left).start()
+
+        @pl.when(relayed)
+        def _():
+            xcopy(buf, ph, 5, j, bot, right, left).start()
+
         xcopy(buf, ph, 6, j, allr, right, sib).start()
 
     def send_far(buf, ph, j):
         allr, top, bot = parts_of(buf)
-        xcopy(buf, ph, 3, j, top, across, right).wait_recv()
-        xcopy(buf, ph, 5, j, bot, across, left).wait_recv()
+
+        @pl.when(straight(ph, j))
+        def _():
+            xcopy(buf, ph, 3, j, allr, across, across).wait_recv()
+
+        @pl.when(jnp.logical_not(straight(ph, j)))
+        def _():
+            xcopy(buf, ph, 3, j, top, across, right).wait_recv()
+            xcopy(buf, ph, 5, j, bot, across, left).wait_recv()
+
         xcopy(buf, ph, 7, j, allr, across, sib).start()
 
     def all_in(buf, ph, j):
@@ -183,17 +221,25 @@
 
     def all_sent(buf, ph, j):
         allr, top, bot = parts_of(buf)
-        for kind in range(8):
-            part = top if kind == 3 else bot if kind == 5 else allr
-            xcopy(buf, ph, kind, j, part, tp, right).wait_send()
+        for kind in (0, 1, 2, 4, 6, 7):
+            xcopy(buf, ph, kind, j, allr, tp, right).wait_send()
+
+        @pl.when(straight(ph, j))
+        def _():
+            xcopy(buf, ph, 3, j, allr, tp, across).wait_send()
+
+        @pl.when(jnp.logical_not(straight(ph, j)))
+        def _():
+            xcopy(buf, ph, 3, j, top, left, right).wait_send()
+            xcopy(buf, ph, 5, j, bot, right, left).wait_send()
 
     pl.semaphore_wait(barrier, NZ * NY - 1 + NTP - 1)
     send_own(toks, 2, 0)
 
     for b in range(NTP):
         gain_pad[:, b * PAD + 2 * LANES : (b + 1) * PAD] = jnp.zeros((1, LANES), F32)
-        gain_pad[:, b * PAD : b * PAD + COL] = again[:, b * COL : (b + 1) * COL]
-        own = mgain[:, b * COL : (b + 1) * COL]
+        gain_pad[:, b * PAD : b * PAD + COL] = gains[0:1, b * COL : (b + 1) * COL]
+        own = gains[1:2, b * COL : (b + 1) * COL]
 
         @pl.when(tp == b)
         def _():
@@ -212,7 +258,8 @@
     table[0] = jnp.cos(angles)
     sine = jnp.sin(angles)
     table[1] = jnp.where(first, -sine, sine)
-    table[2] = pos_col
+    for g in range(8):
+        posb[pl.ds(g, TOK, stride=8), :] = pos_col
 
     experts = NZ * NY
     e_iota = lax.broadcasted_iota(jnp.int32, (experts, TOK), 0)
@@ -224,6 +271,8 @@
         < lax.broadcasted_iota(jnp.int32, (TOK, TOK), 1)
     ).astype(F32)
     named_f = named.astype(F32)
+    router_pad[...] = jnp.zeros((experts, PAD), BF)
+    router_pad[:, :COL] = router_t[...]
     slot = jnp.dot(named_f, before, preferred_element_type=F32)
     slot = jnp.where(named, slot, -1.0)
     s_iota = lax.broadcasted_iota(jnp.int32, (SLOTS, TOK), 0).astype(F32)
@@ -233,15 +282,7 @@
         ).astype(F32)
 
     send_on(toks, 2, 0)
-    for u, get in enumerate(get_gu):
-        get.wait()
-    raw_gu[COL:PAD, :] = jnp.zeros((PAD - COL, FULL), BF)
-    raw_gu[PAD + COL : 2 * PAD, :] = jnp.zeros((PAD - COL, FULL), BF)
-    spread_blocks(raw_gu, wgu, 2 * PAD, 48)
     send_far(toks, 2, 0)
-    get_dn.wait()
-    raw_dn[COL:PAD, :] = jnp.zeros((PAD - COL, FULL), BF)
-    spread_blocks(raw_dn, wdn, PAD, 48)
     for group, ref in ((get_q, wq), (get_kv, wkv), (get_o, wo)):
         for b, get in enumerate(group):
             get.wait()
@@ -272,42 +313,53 @@
         kvb[pl.ds(g, TOK, stride=8), :] = entry
     get_cache.wait()
 
-    def score(n, c):
-        for u in range(8):
-            s = n * 8 + u
-            at = pl.ds(pl.multiple_of(s * 8, 8), 8)
-            scb[at, :] = dot_nt(qbuf[at, :].astype(BF), cache[s])
-        return c
-
-    lax.fori_loop(0, TOK // 8, score, 0)
     sub = lax.broadcasted_iota(jnp.int32, (8, LANES), 0)
     sink = jnp.where(
         sub == 0,
         sinks[0],
         jnp.where(sub == 1, sinks[1], jnp.where(sub == 2, sinks[2], sinks[3])),
     )[:, :1]
-    slots = lax.broadcasted_iota(jnp.int32, (8, LANES), 1)
-
-    def soften(n, c):
-        for u in range(8):
-            s = n * 8 + u
-            at = pl.ds(pl.multiple_of(s * 8, 8), 8)
-            where_now = table[2, pl.ds(s, 1), :].astype(jnp.int32)
-            current = slots == lax.rem(where_now, LANES)
-            newest = jnp.sum(qbuf[at, :] * kvb[at, :], axis=1, keepdims=True)
-            raw = jnp.where(current, newest, scb[at, :])
-            raw = jnp.where(slots <= where_now, raw, -jnp.inf)
-            peak = jnp.maximum(jnp.max(raw, axis=1, keepdims=True), sink)
-            raised = jnp.exp(raw - peak)
-            total = jnp.sum(raised, axis=1, keepdims=True) + jnp.exp(sink - peak)
-            probs = (raised / total).astype(BF)
-            newest_prob = (jnp.exp(newest - peak) / total).astype(BF).astype(F32)
-            kept = jnp.where(current, 0.0, probs.astype(F32)).astype(BF)
-            mixed = jnp.dot(kept, cache[s], preferred_element_type=F32)
-            scb[at, :] = mixed + newest_prob * kvb[at, :]
+    group = 24
+    sink = jnp.concatenate([sink] * group, axis=0)
+    slots = lax.broadcasted_iota(jnp.int32, (8 * group, LANES), 1)
+
+    def attend(n, c):
+        at = pl.ds(pl.multiple_of(n * 8 * group, 8 * group), 8 * group)
+        asked = qbuf[at, :]
+        entries = kvb[at, :]
+        where_now = posb[at, :].astype(jnp.int32)
+        newest = jnp.sum(asked * entries, axis=1, keepdims=True)
+        raw = jnp.concatenate(
+            [
+                dot_nt(asked[8 * u : 8 * u + 8].astype(BF), cache[n * group + u])
+                for u in range(group)
+            ],
+            axis=0,
+        )
+        current = slots == lax.rem(where_now, LANES)
+        raw = jnp.where(current, newest, raw)
+        raw = jnp.where(slots <= where_now, raw, -jnp.inf)
+        peak = jnp.maximum(jnp.max(raw, axis=1, keepdims=True), sink)
+        raised = jnp.exp(raw - peak)
+        total = jnp.sum(raised, axis=1, keepdims=True) + jnp.exp(sink - peak)
+        probs = (raised / total).astype(BF).astype(F32)
+        newest_prob = (jnp.exp(newest - peak) / total).astype(BF).astype(F32)
+        kept = jnp.where(current, 0.0, probs)
+        mixed = jnp.concatenate(
+            [
+                jnp.dot(
+                    kept[8 * u : 8 * u + 8].astype(BF),
+                    cache[n * group + u],
+                    preferred_element_type=F32,
+                )
+                for u in range(group)
+            ],
+            axis=0,
+        )
+        scb[at, :] = mixed + newest_prob * entries
         return c
 
-    lax.fori_loop(0, TOK // 8, soften, 0)
+    lax.fori_loop(0, TOK // group, attend, 0)
     tiles = []
     for tile in range(2):
         even = scb[pl.ds(2 * tile, TOK, stride=8), :]
@@ -349,44 +401,21 @@
         chip_b[owner] = (mine_f[owner] + sib_b[owner].astype(F32)).astype(BF)
         to_chip(i).start()
     total = tok_pad[...] + (mine_f[xx] + sib_b[xx].astype(F32))
+    for get in get_gu:
+        get.wait()
+    raw_gu[COL:PAD, :] = jnp.zeros((PAD - COL, FULL), BF)
+    raw_gu[PAD + COL : 2 * PAD, :] = jnp.zeros((PAD - COL, FULL), BF)
+    spread_blocks(raw_gu, wgu, 2 * PAD, 48)
+    get_dn.wait()
+    raw_dn[COL:PAD, :] = jnp.zeros((PAD - COL, FULL), BF)
+    spread_blocks(raw_dn, wdn, PAD, 48)
     for i in (1, 3, 2):
         to_chip(i).wait_recv()
     for i in (1, 2, 3):
         total = total + recv_b[i].astype(F32)
     resid[...] = total
 
-    lifted = total * own_gain[...]
-    wide_rows = jnp.zeros((LANES - TOK, PAD), BF)
-    logit_part = jnp.zeros((experts, LANES), F32)
-    for piece in split3(lifted):
-        logit_part = logit_part + dot_nt(router_t[...], jnp.concatenate([piece, wide_rows], axis=0))
-    square_part = jnp.zeros((8, LANES), F32)
-    ones = jnp.ones((8, PAD), BF)
-    for piece in split3(total * total):
-        square_part = square_part + dot_nt(ones, jnp.concatenate([piece, wide_rows], axis=0))
-    small_t[tp, 0:experts, :] = logit_part
-    small_t[tp, experts : experts + 8, :] = square_part
-
-    def share(i):
-        return pltpu.make_async_remote_copy(
-            src_ref=small_t.at[tp],
-            dst_ref=small_t.at[tp],
-            send_sem=a_send.at[i],
-            recv_sem=a_recv.at[i],
-            device_id=(dp, lax.rem(tp + i, NTP)),
-            device_id_type=MESH,
-        )
-
-    for i in range(1, NTP):
-        share(i).start()
-    for i in range(1, NTP):
-        share(i).wait_recv()
-    summed = small_t[0]
-    for n in range(1, NTP):
-        summed = summed + small_t[n]
-    scale_row = lax.rsqrt(summed[experts : experts + 1, :] * (1.0 / FULL) + norm_eps)
-    scale_col = jnp.transpose(jnp.broadcast_to(scale_row, (LANES, LANES)))[:TOK, :1]
-    hid[...] = (resid[...] * scale_col * own_gain[...]).astype(BF)
+    hid[...] = (total * own_gain[...]).astype(BF)
 
     def dispatch_copy(j, i):
         dest = lax.rem(z + NZ + NZ - z_offset(j), NZ) * NY + lax.rem(y + NY - i, NY)
@@ -401,7 +430,7 @@
 
     own_in = pltpu.make_async_copy(
         placed.at[pl.ds(pl.multiple_of(dp * SLOTS, SLOTS), SLOTS), :],
-        rows.at[0, pl.ds(0, SLOTS), cols(tp)],
+        rows.at[OWN, pl.ds(0, SLOTS), cols(tp)],
         lsem.at[0],
     )
 
@@ -412,11 +441,11 @@
             placer[part, :].astype(BF), hid[...], preferred_element_type=F32
         ).astype(BF)
 
-        @pl.when(j == 0)
+        @pl.when(j == OWN)
         def _():
             own_in.start()
 
-        @pl.when(j > 0)
+        @pl.when(j != OWN)
         def _():
             dispatch_copy(j, 0).start()
 
@@ -424,20 +453,112 @@
             dispatch_copy(j, i).start()
         return c
 
-    lax.fori_loop(0, NZ, dispatch, 0)
-
-    logits = summed[0:experts, :TOK] * scale_row[:, :TOK]
-    lifted_logits = jnp.where(named, jnp.exp(logits), 0.0)
-    weights = lifted_logits / jnp.sum(lifted_logits, axis=0, keepdims=True)
-    for e in range(experts):
-        at = slice(e * SLOTS, (e + 1) * SLOTS)
-        placer[at, :] = placer[at, :] * weights[e : e + 1, :]
-    for n in range(NZ):
-        at = slice(n * CHUNK, (n + 1) * CHUNK)
-        piece = jnp.transpose(placer[at, :])
-        hi = piece.astype(BF)
-        comb_hi[:, at] = hi
-        comb_lo[:, at] = (piece - hi.astype(F32)).astype(BF)
+    lifted = total * own_gain[...]
+    wide_rows = jnp.zeros((LANES - TOK, PAD), BF)
+    logit_part = jnp.zeros((experts, LANES), F32)
+    for piece in split3(lifted):
+        logit_part = logit_part + dot_nt(router_pad[...], jnp.concatenate([piece, wide_rows], axis=0))
+    square_part = jnp.zeros((8, LANES), F32)
+    ones = jnp.ones((8, PAD), BF)
+    for piece in split3(total * total):
+        square_part = square_part + dot_nt(ones, jnp.concatenate([piece, wide_rows], axis=0))
+    small_t[tp, 0:experts, :] = logit_part
+    small_t[tp, experts : experts + 8, :] = square_part
+
+    def share(i):
+        return pltpu.make_async_remote_copy(
+            src_ref=small_t.at[tp],
+            dst_ref=small_t.at[tp],
+            send_sem=a_send.at[i],
+            recv_sem=a_recv.at[i],
+            device_id=(dp, lax.rem(tp + i, NTP)),
+            device_id_type=MESH,
+        )
+
+    for i in range(1, NTP):
+        share(i).start()
+
+
+    lax.fori_loop(0, AHEAD, dispatch, 0)
+
+    def scale_copy(j, i):
+        zd = lax.rem(z + NZ - z_offset(j), NZ)
+        dest = zd * NY + lax.rem(y + NY - i, NY)
+        return pltpu.make_async_remote_copy(
+            src_ref=scale_out.at[zd],
+            dst_ref=scale_in.at[j * NY + i],
+            send_sem=s_send.at[j * NY + i],
+            recv_sem=s_recv.at[j * NY + i],
+            device_id=(dest, tp),
+            device_id_type=MESH,
+        )
+
+    def scales_of(j):
+        spot = lax.broadcasted_iota(jnp.int32, (1, LANES), 1)
+        line = jnp.zeros((1, LANES), F32)
+        for i in range(NY):
+
+            @pl.when((j != OWN) | (i != 0))
+            def _():
+                scale_copy(j, i).wait_recv()
+
+            there = pltpu.roll(
+                jnp.broadcast_to(scale_in[j * NY + i], (8, LANES)),
+                lax.rem(i + NY - y, NY) * SLOTS,
+                axis=1,
+            )[0:1]
+            line = jnp.where(lax.div(spot, SLOTS) == i, there, line)
+        return jnp.transpose(jnp.broadcast_to(line, (LANES, LANES)))[:, :1]
+
+    def sums():
+        summed = small_t[0]
+        for n in range(1, NTP):
+            summed = summed + small_t[n]
+        scale_row = lax.rsqrt(summed[experts : experts + 1, :] * (1.0 / FULL) + norm_eps)
+        return summed, scale_row
+
+    def settle():
+        for i in range(1, NTP):
+            share(i).wait_recv()
+        scale_row = sums()[1]
+        hi, mid, low = split3(jnp.broadcast_to(scale_row[:, :TOK], (8, TOK)))
+        which = lax.broadcasted_iota(jnp.int32, (8, TOK), 0)
+        stacked = jnp.where(
+            which == 0,
+            hi.astype(F32),
+            jnp.where(which == 1, mid.astype(F32), jnp.where(which == 2, low.astype(F32), 0.0)),
+        ).astype(BF)
+        for n in range(NZ):
+            at = slice(n * CHUNK, (n + 1) * CHUNK)
+            spots = placer[at, :].astype(BF)
+            scale_out[n] = jnp.sum(dot_nt(stacked, spots), axis=0, keepdims=True)
+        scale_in[OWN * NY] = scale_out[z]
+
+        def send_scale(n, c):
+            j, i = lax.div(n, NY), lax.rem(n, NY)
+
+            @pl.when(n != OWN * NY)
+            def _():
+                scale_copy(j, i).start()
+
+            return c
+
+        lax.fori_loop(0, NZ * NY, send_scale, 0)
+
+    def combine_weights():
+        summed, scale_row = sums()
+        logits = summed[0:experts, :TOK] * scale_row[:, :TOK]
+        lifted_logits = jnp.where(named, jnp.exp(logits), 0.0)
+        weights = lifted_logits / jnp.sum(lifted_logits, axis=0, keepdims=True)
+        for e in range(experts):
+            at = slice(e * SLOTS, (e + 1) * SLOTS)
+            placer[at, :] = placer[at, :] * weights[e : e + 1, :]
+        for n in range(NZ):
+            at = slice(n * CHUNK, (n + 1) * CHUNK)
+            piece = jnp.transpose(placer[at, :])
+            hi = piece.astype(BF)
+            comb_hi[:, at] = hi
+            comb_lo[:, at] = (piece - hi.astype(F32)).astype(BF)
 
     def back_copy(j, i):
         home = lax.rem(z + z_offset(j), NZ) * NY + lax.rem(y + i, NY)
@@ -451,19 +572,23 @@
         )
 
     own_back = pltpu.make_async_copy(
-        made.at[0, pl.ds(0, SLOTS), :],
+        made.at[OWN, pl.ds(0, SLOTS), :],
         back.at[pl.ds(pl.multiple_of(dp * SLOTS, SLOTS), SLOTS), :],
         lsem.at[1],
     )
 
     def step(t, c):
+        @pl.when((t >= 2) & (t < NZ + 2))
+        def _():
+            send_far(rows, 0, t - 2)
+
         @pl.when(t < NZ)
         def _():
-            @pl.when(t == 0)
+            @pl.when(t == OWN)
             def _():
                 own_in.wait()
 
-            @pl.when(t > 0)
+            @pl.when(t != OWN)
             def _():
                 dispatch_copy(t, 0).wait_recv()
 
@@ -471,44 +596,53 @@
                 dispatch_copy(t, i).wait_recv()
             send_own(rows, 0, t)
 
+        @pl.when(t == 0)
+        def _():
+            settle()
+
         @pl.when((t >= 1) & (t < NZ + 1))
         def _():
             send_on(rows, 0, t - 1)
 
+        @pl.when(t < NZ - AHEAD)
+        def _():
+            dispatch(t + AHEAD, 0)
+
         @pl.when((t >= 2) & (t < NZ + 2))
         def _():
-            send_far(rows, 0, t - 2)
-
-        @pl.when((t >= 3) & (t < NZ + 3))
-        def _():
-            j = t - 3
+            j = t - 2
+            scales = scales_of(j)
             all_in(rows, 0, j)
-            mixed = dot_nt(rows[j], wgu[...])
+            mixed = dot_nt(rows[j], wgu[...]) * scales
             gate = mixed[:, :PAD]
             up = mixed[:, PAD:]
             act = gate * jax.nn.sigmoid(glu_alpha * gate) * (up + 1.0)
             acts[j, :, cols(tp)] = act.astype(BF)
             send_own(acts, 1, j)
 
-        @pl.when((t >= 4) & (t < NZ + 4))
-        def _():
-            send_on(acts, 1, t - 4)
-
-        @pl.when((t >= 5) & (t < NZ + 5))
-        def _():
-            send_far(acts, 1, t - 5)
-
-        @pl.when(t >= 6)
-        def _():
-            j = t - 6
+        @pl.when(t >= 4)
+        def _():
+            send_far(acts, 1, t - 4)
+
+        @pl.when((t >= 3) & (t < NZ + 3))
+        def _():
+            send_on(acts, 1, t - 3)
+
+        @pl.when(t == NZ - AHEAD + 1)
+        def _():
+            combine_weights()
+
+        @pl.when(t >= 4)
+        def _():
+            j = t - 4
             all_in(acts, 1, j)
             made[j] = dot_nt(acts[j], wdn[...]).astype(BF)
 
-            @pl.when(j == 0)
+            @pl.when(j == OWN)
             def _():
                 own_back.start()
 
-            @pl.when(j > 0)
+            @pl.when(j != OWN)
             def _():
                 back_copy(j, 0).start()
 
@@ -517,7 +651,7 @@
 
         return c
 
-    lax.fori_loop(0, NZ + 6, step, 0)
+    lax.fori_loop(0, NZ + 4, step, 0)
 
     def await_back(i, c):
         peer = lax.rem(dp + i, NZ * NY)
@@ -549,11 +683,16 @@
     all_sent(toks, 2, 0)
 
     def sent(n, c):
-        dispatch_copy(lax.div(n, NY), lax.rem(n, NY)).wait_send()
-        back_copy(lax.div(n, NY), lax.rem(n, NY)).wait_send()
+        @pl.when(n != OWN * NY)
+        def _():
+            j, i = lax.div(n, NY), lax.rem(n, NY)
+            dispatch_copy(j, i).wait_send()
+            back_copy(j, i).wait_send()
+            scale_copy(j, i).wait_send()
+
         return c
 
-    lax.fori_loop(1, NZ * NY, sent, 0)
+    lax.fori_loop(0, NZ * NY, sent, 0)
 
     def sent_x(j, c):
         all_sent(rows, 0, j)
@@ -583,11 +722,10 @@
     hbm = pl.BlockSpec(memory_space=pl.ANY)
     dma = pltpu.SemaphoreType.DMA
     vm = pltpu.VMEM
-    router_t = jnp.pad(jnp.transpose(router), ((0, 0), (0, PAD - COL)))
     return pl.pallas_call(
         layer_body,
         out_shape=jax.ShapeDtypeStruct(tokens.shape, F32),
-        in_specs=[vmem, vmem, vmem, smem, vmem, vmem, vmem] + [hbm] * 6,
+        in_specs=[vmem, vmem, smem, vmem, vmem, vmem] + [hbm] * 6,
         out_specs=vmem,
         scratch_shapes=[
             vm((NZ, CHUNK, WIDE), BF),
@@ -620,9 +758,13 @@
             vm((NX, TOK, PAD), BF),
             vm((NX, TOK, PAD), BF),
             vm((NX, TOK, PAD), BF),
-            vm((3, TOK, LANES), F32),
+            vm((2, TOK, LANES), F32),
             vm((8, LANES), F32),
             vm((NTP, 40, LANES), F32),
+            vm((SPAN, LANES), F32),
+            vm((NZ * NY, PAD), BF),
+            vm((NZ, 1, LANES), F32),
+            vm((NZ * NY, 1, LANES), F32),
             dma((28,)),
             dma((2,)),
             dma((NZ * NY,)),
@@ -635,6 +777,8 @@
             dma((NX,)),
             dma((NTP,)),
             dma((NTP,)),
+            dma((NZ * NY,)),
+            dma((NZ * NY,)),
         ],
         compiler_params=pltpu.CompilerParams(
             collective_id=0, has_side_effects=True, vmem_limit_bytes=60 * 1024 * 1024
@@ -642,11 +786,10 @@
         name="layer",
     )(
         tokens,
-        attn_gain[None, :],
-        moe_gain[None, :],
+        jnp.stack([attn_gain, moe_gain]),
         attn_sinks,
         positions[None, :],
-        router_t,
+        jnp.transpose(router),
         jnp.transpose(expert_ids),
         w_query,
         w_keyvalue.reshape(FULL, 2 * HD),

time: 129 us -> 114 us (0.88)
  Pallas kernels: 123 us -> 110 us
  local copies, waits for them, and re-layouts: 5.55 us -> 3.01 us
    pallas_call x1, Pallas kernels: 123 us -> 110 us  [on_device(): pl.pallas_call(layer_body, out_shape=jax.ShapeDtypeStruct(tokens.shape, F...]
    broadcast_in_dim x2 -> x0, local copies, waits for them, and re-layouts: 2.62 us -> none  [the longest x1 1.31 us: on_device(): moe_gain[None, :]]
    another operation x0 -> x2, local copies, waits for them, and re-layouts: none -> 1.43 us  [on_device(): jnp.stack([attn_gain, moe_gain])]
    pad x1 -> x0, local copies, waits for them, and re-layouts: 1.35 us -> none  [on_device(): router_t = jnp.pad(jnp.transpose(router), ((0, 0), (0, PAD - COL)))]
where the time goes in v2:
time: 114 us; the launch traced here: 113 us
  Pallas kernels  110 us (96%)
  local copies, waits for them, and re-layouts  3.01 us (3%)
    pallas_call x1, Pallas kernels, on_device(): pl.pallas_call(layer_body, out_shape=jax.ShapeDtypeStruct(tokens.shape, F...  110 us

profile of v2, /device:TPU:1, one launch (start us, length us, event | category | flops | bytes accessed | tf_op | source)
XLA Modules:
  0.0 113.5 jit_solution(4871749008029961763)
XLA Ops:
  0.0 0.7 stack.9
  0.7 0.7 stack.10
  1.4 0.6 pad_maximum_fusion.gains
  2.1 109.8 %layer.1 = f32[96,360]{1,0:T(8,128)} custom-call(bf16[96,360]{1,0:T(8,128)(2,1)} %tokens.1, f32[2,2880]{1,0:T(2,128)} %pad_maximum_fusion.gains, f32[4]{0:T(128)} %sinks.1, s32[1,96]{1,0:T(1,128)} %bitcast.19, bf16[32,360]{1,0:T(8,128)(2,1)} %bitcast.17, s32[4,96]{1,0:T(4,128)} %bitcast.18, bf16[2880,256]{1,0:T(8,128)(2,1)} %wq_hbm.1, ...), custom_call_target="tpu_custom_call" | custom-call | tf_op jit(solution)/shard_map/layer/pallas_call | solution.py:725
  111.9 1.6 %copy.15 = f32[96,360]{1,0:T(8,128)} copy(f32[96,360]{1,0:T(8,128)} %layer.1) | data formatting | bytes 276480

commit v3 on v2

--- a/solution.py
+++ b/solution.py
@@ -19,7 +19,11 @@
 NX = 4
 NTP = 2 * NX
 SLOTS = 32
-CHUNK = NY * SLOTS
+GROUP = NY * SLOTS
+PAIR = 4
+CHUNK = PAIR * SLOTS
+PARTS = NY // PAIR
+NC = NZ * PARTS
 WIDE = NTP * PAD
 TOK = 96
 HEADS = 4
@@ -32,11 +36,13 @@
 BF = jnp.bfloat16
 
 
-ORDER = (0, 7, 2, 4, 5, 3, 6, 1)
+ORDER = (0, 1, 2, 4, 5, 3, 6, 7)
 OWN = ORDER.index(0)
+SETTLE = 1
 AHEAD = 3
 STRAIGHT_ROWS = 1
-STRAIGHT_ACTS = 2
+STRAIGHT_ACTS = 0
+ON, FAR, GATE, ACT_ON, ACT_FAR, DOWN = 1, 2, 3, 4, 5, 6
 STRAIGHT_TOKENS = True
 
 
@@ -167,7 +173,7 @@
     def straight(ph, j):
         if ph == 2:
             return STRAIGHT_TOKENS
-        return j < STRAIGHT_ROWS if ph == 0 else j >= NZ - STRAIGHT_ACTS
+        return j < STRAIGHT_ROWS if ph == 0 else j >= NC - STRAIGHT_ACTS
 
     def send_own(buf, ph, j):
         allr, top, bot = parts_of(buf)
@@ -319,7 +325,7 @@
         sinks[0],
         jnp.where(sub == 1, sinks[1], jnp.where(sub == 2, sinks[2], sinks[3])),
     )[:, :1]
-    group = 24
+    group = 48
     sink = jnp.concatenate([sink] * group, axis=0)
     slots = lax.broadcasted_iota(jnp.int32, (8 * group, LANES), 1)
 
@@ -417,11 +423,14 @@
 
     hid[...] = (total * own_gain[...]).astype(BF)
 
+    def within(i):
+        return pl.ds(pl.multiple_of(lax.rem(i, PAIR) * SLOTS, SLOTS), SLOTS)
+
     def dispatch_copy(j, i):
         dest = lax.rem(z + NZ + NZ - z_offset(j), NZ) * NY + lax.rem(y + NY - i, NY)
         return pltpu.make_async_remote_copy(
             src_ref=placed.at[pl.ds(pl.multiple_of(dest * SLOTS, SLOTS), SLOTS), :],
-            dst_ref=rows.at[j, pl.ds(pl.multiple_of(i * SLOTS, SLOTS), SLOTS), cols(tp)],
+            dst_ref=rows.at[j * PARTS + lax.div(i, PAIR), within(i), cols(tp)],
             send_sem=d_send.at[j * NY + i],
             recv_sem=d_recv.at[j * NY + i],
             device_id=(dest, tp),
@@ -430,13 +439,13 @@
 
     own_in = pltpu.make_async_copy(
         placed.at[pl.ds(pl.multiple_of(dp * SLOTS, SLOTS), SLOTS), :],
-        rows.at[OWN, pl.ds(0, SLOTS), cols(tp)],
+        rows.at[OWN * PARTS, pl.ds(0, SLOTS), cols(tp)],
         lsem.at[0],
     )
 
     def dispatch(j, c):
         zd = lax.rem(z + NZ + NZ - z_offset(j), NZ)
-        part = pl.ds(pl.multiple_of(zd * CHUNK, CHUNK), CHUNK)
+        part = pl.ds(pl.multiple_of(zd * GROUP, GROUP), GROUP)
         placed[part, :] = jnp.dot(
             placer[part, :].astype(BF), hid[...], preferred_element_type=F32
         ).astype(BF)
@@ -493,22 +502,23 @@
             device_id_type=MESH,
         )
 
-    def scales_of(j):
+    def scales_of(c):
         spot = lax.broadcasted_iota(jnp.int32, (1, LANES), 1)
         line = jnp.zeros((1, LANES), F32)
-        for i in range(NY):
-
-            @pl.when((j != OWN) | (i != 0))
+        for k in range(PAIR):
+            n = c * PAIR + k
+
+            @pl.when(n != OWN * NY)
             def _():
-                scale_copy(j, i).wait_recv()
+                scale_copy(lax.div(n, NY), lax.rem(n, NY)).wait_recv()
 
             there = pltpu.roll(
-                jnp.broadcast_to(scale_in[j * NY + i], (8, LANES)),
-                lax.rem(i + NY - y, NY) * SLOTS,
+                jnp.broadcast_to(scale_in[n], (8, LANES)),
+                lax.rem(k + NY - y, NY) * SLOTS,
                 axis=1,
             )[0:1]
-            line = jnp.where(lax.div(spot, SLOTS) == i, there, line)
-        return jnp.transpose(jnp.broadcast_to(line, (LANES, LANES)))[:, :1]
+            line = jnp.where(lax.div(spot, SLOTS) == k, there, line)
+        return jnp.transpose(jnp.broadcast_to(line, (LANES, LANES)))[:CHUNK, :1]
 
     def sums():
         summed = small_t[0]
@@ -529,7 +539,7 @@
             jnp.where(which == 1, mid.astype(F32), jnp.where(which == 2, low.astype(F32), 0.0)),
         ).astype(BF)
         for n in range(NZ):
-            at = slice(n * CHUNK, (n + 1) * CHUNK)
+            at = slice(n * GROUP, (n + 1) * GROUP)
             spots = placer[at, :].astype(BF)
             scale_out[n] = jnp.sum(dot_nt(stacked, spots), axis=0, keepdims=True)
         scale_in[OWN * NY] = scale_out[z]
@@ -554,7 +564,7 @@
             at = slice(e * SLOTS, (e + 1) * SLOTS)
             placer[at, :] = placer[at, :] * weights[e : e + 1, :]
         for n in range(NZ):
-            at = slice(n * CHUNK, (n + 1) * CHUNK)
+            at = slice(n * GROUP, (n + 1) * GROUP)
             piece = jnp.transpose(placer[at, :])
             hi = piece.astype(BF)
             comb_hi[:, at] = hi
@@ -563,7 +573,7 @@
     def back_copy(j, i):
         home = lax.rem(z + z_offset(j), NZ) * NY + lax.rem(y + i, NY)
         return pltpu.make_async_remote_copy(
-            src_ref=made.at[j, pl.ds(pl.multiple_of(i * SLOTS, SLOTS), SLOTS), :],
+            src_ref=made.at[j * PARTS + lax.div(i, PAIR), within(i), :],
             dst_ref=back.at[pl.ds(pl.multiple_of(dp * SLOTS, SLOTS), SLOTS), :],
             send_sem=r_send.at[j * NY + i],
             recv_sem=r_recv.at[dp],
@@ -572,45 +582,42 @@
         )
 
     own_back = pltpu.make_async_copy(
-        made.at[OWN, pl.ds(0, SLOTS), :],
+        made.at[OWN * PARTS, pl.ds(0, SLOTS), :],
         back.at[pl.ds(pl.multiple_of(dp * SLOTS, SLOTS), SLOTS), :],
         lsem.at[1],
     )
 
     def step(t, c):
-        @pl.when((t >= 2) & (t < NZ + 2))
-        def _():
-            send_far(rows, 0, t - 2)
-
-        @pl.when(t < NZ)
-        def _():
-            @pl.when(t == OWN)
-            def _():
-                own_in.wait()
-
-            @pl.when(t != OWN)
-            def _():
-                dispatch_copy(t, 0).wait_recv()
-
-            for i in range(1, NY):
-                dispatch_copy(t, i).wait_recv()
+        @pl.when(t < NC)
+        def _():
+            for k in range(PAIR):
+                n = t * PAIR + k
+
+                @pl.when(n == OWN * NY)
+                def _():
+                    own_in.wait()
+
+                @pl.when(n != OWN * NY)
+                def _():
+                    dispatch_copy(lax.div(n, NY), lax.rem(n, NY)).wait_recv()
+
             send_own(rows, 0, t)
 
-        @pl.when(t == 0)
+        @pl.when(t == SETTLE)
         def _():
             settle()
 
-        @pl.when((t >= 1) & (t < NZ + 1))
-        def _():
-            send_on(rows, 0, t - 1)
-
-        @pl.when(t < NZ - AHEAD)
-        def _():
-            dispatch(t + AHEAD, 0)
-
-        @pl.when((t >= 2) & (t < NZ + 2))
-        def _():
-            j = t - 2
+        @pl.when((t >= ON) & (t < NC + ON))
+        def _():
+            send_on(rows, 0, t - ON)
+
+        @pl.when((lax.rem(t, PARTS) == 0) & (t < (NZ - AHEAD) * PARTS))
+        def _():
+            dispatch(lax.div(t, PARTS) + AHEAD, 0)
+
+        @pl.when((t >= GATE) & (t < NC + GATE))
+        def _():
+            j = t - GATE
             scales = scales_of(j)
             all_in(rows, 0, j)
             mixed = dot_nt(rows[j], wgu[...]) * scales
@@ -620,38 +627,67 @@
             acts[j, :, cols(tp)] = act.astype(BF)
             send_own(acts, 1, j)
 
-        @pl.when(t >= 4)
-        def _():
-            send_far(acts, 1, t - 4)
-
-        @pl.when((t >= 3) & (t < NZ + 3))
-        def _():
-            send_on(acts, 1, t - 3)
-
-        @pl.when(t == NZ - AHEAD + 1)
+        @pl.when((t >= FAR) & (t < NC + FAR))
+        def _():
+            send_far(rows, 0, t - FAR)
+
+        @pl.when((t >= ACT_ON) & (t < NC + ACT_ON))
+        def _():
+            send_on(acts, 1, t - ACT_ON)
+
+        @pl.when(t == (NZ - AHEAD) * PARTS + 1)
         def _():
             combine_weights()
 
-        @pl.when(t >= 4)
-        def _():
-            j = t - 4
+        @pl.when((t >= DOWN) & (t < NC + DOWN))
+        def _():
+            j = t - DOWN
             all_in(acts, 1, j)
             made[j] = dot_nt(acts[j], wdn[...]).astype(BF)
-
-            @pl.when(j == OWN)
-            def _():
-                own_back.start()
-
-            @pl.when(j != OWN)
-            def _():
-                back_copy(j, 0).start()
-
-            for i in range(1, NY):
-                back_copy(j, i).start()
+            for k in range(PAIR):
+                n = j * PAIR + k
+
+                @pl.when(n == OWN * NY)
+                def _():
+                    own_back.start()
+
+                @pl.when(n != OWN * NY)
+                def _():
+                    back_copy(lax.div(n, NY), lax.rem(n, NY)).start()
+
+        @pl.when((t >= ACT_FAR) & (t < NC + ACT_FAR))
+        def _():
+            send_far(acts, 1, t - ACT_FAR)
 
         return c
 
-    lax.fori_loop(0, NZ + 4, step, 0)
+    lax.fori_loop(0, NC + DOWN, step, 0)
+
+    to_sib.wait_send()
+    for i in range(1, NX):
+        to_chip(i).wait_send()
+    for i in range(1, NTP):
+        share(i).wait_send()
+    all_sent(toks, 2, 0)
+
+    def sent(n, c):
+        @pl.when(n != OWN * NY)
+        def _():
+            j, i = lax.div(n, NY), lax.rem(n, NY)
+            dispatch_copy(j, i).wait_send()
+            back_copy(j, i).wait_send()
+            scale_copy(j, i).wait_send()
+
+        return c
+
+    lax.fori_loop(0, NZ * NY, sent, 0)
+
+    def sent_x(j, c):
+        all_sent(rows, 0, j)
+        all_sent(acts, 1, j)
+        return c
+
+    lax.fori_loop(0, NC, sent_x, 0)
 
     def await_back(i, c):
         peer = lax.rem(dp + i, NZ * NY)
@@ -674,32 +710,6 @@
         + jnp.dot(comb_lo[...], got, preferred_element_type=F32)
     )
     out[...] = answer[:, :COL]
-
-    to_sib.wait_send()
-    for i in range(1, NX):
-        to_chip(i).wait_send()
-    for i in range(1, NTP):
-        share(i).wait_send()
-    all_sent(toks, 2, 0)
-
-    def sent(n, c):
-        @pl.when(n != OWN * NY)
-        def _():
-            j, i = lax.div(n, NY), lax.rem(n, NY)
-            dispatch_copy(j, i).wait_send()
-            back_copy(j, i).wait_send()
-            scale_copy(j, i).wait_send()
-
-        return c
-
-    lax.fori_loop(0, NZ * NY, sent, 0)
-
-    def sent_x(j, c):
-        all_sent(rows, 0, j)
-        all_sent(acts, 1, j)
-        return c
-
-    lax.fori_loop(0, NZ, sent_x, 0)
 
 
 def on_device(
@@ -728,13 +738,13 @@
         in_specs=[vmem, vmem, smem, vmem, vmem, vmem] + [hbm] * 6,
         out_specs=vmem,
         scratch_shapes=[
-            vm((NZ, CHUNK, WIDE), BF),
-            vm((NZ, CHUNK, WIDE), BF),
+            vm((NC, CHUNK, WIDE), BF),
+            vm((NC, CHUNK, WIDE), BF),
             vm((2 * PAD, WIDE), BF),
             vm((PAD, WIDE), BF),
-            vm((NZ * CHUNK, PAD), BF),
-            vm((NZ, CHUNK, PAD), BF),
-            vm((NZ * CHUNK, PAD), BF),
+            vm((NZ * GROUP, PAD), BF),
+            vm((NC, CHUNK, PAD), BF),
+            vm((NZ * GROUP, PAD), BF),
             vm((1, TOK, WIDE), BF),
             vm((WIDE, HEADS * HD), BF),
             vm((WIDE, 2 * HD), BF),
@@ -750,9 +760,9 @@
             vm((SPAN, LANES), F32),
             vm((TOK, PAD), F32),
             vm((TOK, PAD), BF),
-            vm((NZ * CHUNK, TOK), F32),
-            vm((TOK, NZ * CHUNK), BF),
-            vm((TOK, NZ * CHUNK), BF),
+            vm((NZ * GROUP, TOK), F32),
+            vm((TOK, NZ * GROUP), BF),
+            vm((TOK, NZ * GROUP), BF),
             vm((NX, TOK, PAD), F32),
             vm((NX, TOK, PAD), BF),
             vm((NX, TOK, PAD), BF),
@@ -771,8 +781,8 @@
             dma((NZ * NY,)),
             dma((NZ * NY,)),
             dma((NZ * NY,)),
-            dma((3, 8, NZ)),
-            dma((3, 8, NZ)),
+            dma((3, 8, NC)),
+            dma((3, 8, NC)),
             dma((NX,)),
             dma((NX,)),
             dma((NTP,)),

time: 114 us -> 111 us (0.974)
  Pallas kernels: 110 us -> 107 us
    pallas_call x1, Pallas kernels: 110 us -> 107 us  [on_device(): pl.pallas_call(layer_body, out_shape=jax.ShapeDtypeStruct(tokens.shape, F...]
where the time goes in v3:
time: 111 us
  Pallas kernels  107 us (96%)
  local copies, waits for them, and re-layouts  3.01 us (3%)
    pallas_call x1, Pallas kernels, on_device(): pl.pallas_call(layer_body, out_shape=jax.ShapeDtypeStruct(tokens.shape, F...  107 us

profile of v3, /device:TPU:1, one launch (start us, length us, event | category | flops | bytes accessed | tf_op | source)
XLA Modules:
  0.0 110.8 jit_solution(7342592812833569322)
XLA Ops:
  0.0 0.7 stack.9
  0.7 0.7 stack.10
  1.4 0.6 pad_maximum_fusion.gains
  2.1 107.1 %layer.1 = f32[96,360]{1,0:T(8,128)} custom-call(bf16[96,360]{1,0:T(8,128)(2,1)} %tokens.1, f32[2,2880]{1,0:T(2,128)} %pad_maximum_fusion.gains, f32[4]{0:T(128)} %sinks.1, s32[1,96]{1,0:T(1,128)} %bitcast.19, bf16[32,360]{1,0:T(8,128)(2,1)} %bitcast.17, s32[4,96]{1,0:T(4,128)} %bitcast.18, bf16[2880,256]{1,0:T(8,128)(2,1)} %wq_hbm.1, ...), custom_call_target="tpu_custom_call" | custom-call | tf_op jit(solution)/shard_map/layer/pallas_call | solution.py:735
  109.2 1.6 %copy.15 = f32[96,360]{1,0:T(8,128)} copy(f32[96,360]{1,0:T(8,128)} %layer.1) | data formatting | bytes 276480

commit v4 on v3

--- a/solution.py
+++ b/solution.py
@@ -81,12 +81,12 @@
 
 
 def layer_body(
-    tokens, gains, sinks, pos, router_t, ids_t,
+    tokens_hbm, again_hbm, mgain_hbm, sinks_hbm, pos_hbm, router_hbm, ids_hbm,
     wq_hbm, wkv_hbm, wo_hbm, cache_hbm, gu_hbm, dn_hbm,
     out,
     rows, acts, wgu, wdn, placed, made, back,
     toks, wq, wkv, wo, cache, raw_gu, raw_dn,
-    gain_pad, own_gain, tok_pad, qbuf, kvb, scb, resid, hid, placer, comb_hi, comb_lo,
+    tokens, again, mgain, sinks, pos, router_t, ids_t, gain_pad, own_gain, tok_pad, qbuf, kvb, scb, resid, hid, placer, comb_hi, comb_lo,
     mine_f, mine_b, sib_b, chip_b, recv_b, table, small, small_t, posb, router_pad, scale_out, scale_in,
     wsem, lsem, d_send, d_recv, r_send, r_recv, x_send, x_recv,
     o_send, o_recv, a_send, a_recv, s_send, s_recv,
@@ -120,6 +120,22 @@
         )
         return c
 
+    get_small = [
+        pltpu.make_async_copy(source, target, wsem.at[28 + n])
+        for n, (source, target) in enumerate(
+            (
+                (tokens_hbm, tokens),
+                (pos_hbm, pos),
+                (ids_hbm, ids_t),
+                (again_hbm, again),
+                (mgain_hbm, mgain),
+                (router_hbm, router_t),
+                (sinks_hbm, sinks),
+            )
+        )
+    ]
+    for get in get_small:
+        get.start()
     lax.fori_loop(1, NTP, greet_tp, 0)
     lax.fori_loop(1, NZ * NY, greet, 0)
 
@@ -152,6 +168,7 @@
             get.start()
 
     tok_pad[...] = jnp.zeros((TOK, PAD), F32)
+    get_small[0].wait()
     tok_pad[:, :COL] = tokens[...].astype(F32)
     toks[0, :, cols(tp)] = tok_pad[...].astype(BF)
 
@@ -242,10 +259,13 @@
     pl.semaphore_wait(barrier, NZ * NY - 1 + NTP - 1)
     send_own(toks, 2, 0)
 
+    for get in get_small[1:]:
+        get.wait()
+
     for b in range(NTP):
         gain_pad[:, b * PAD + 2 * LANES : (b + 1) * PAD] = jnp.zeros((1, LANES), F32)
-        gain_pad[:, b * PAD : b * PAD + COL] = gains[0:1, b * COL : (b + 1) * COL]
-        own = gains[1:2, b * COL : (b + 1) * COL]
+        gain_pad[:, b * PAD : b * PAD + COL] = again[b * COL : (b + 1) * COL][None, :]
+        own = mgain[b * COL : (b + 1) * COL][None, :]
 
         @pl.when(tp == b)
         def _():
@@ -329,6 +349,16 @@
     sink = jnp.concatenate([sink] * group, axis=0)
     slots = lax.broadcasted_iota(jnp.int32, (8 * group, LANES), 1)
 
+    empty = jnp.zeros((8, LANES), F32)
+
+    def apart(two):
+        upper = jnp.concatenate([two[:8], empty], axis=1)
+        lower = jnp.concatenate([empty, two[8:]], axis=1)
+        return jnp.concatenate([upper, lower], axis=0).astype(BF)
+
+    def both(s):
+        return jnp.concatenate([cache[s], cache[s + 1]], axis=1)
+
     def attend(n, c):
         at = pl.ds(pl.multiple_of(n * 8 * group, 8 * group), 8 * group)
         asked = qbuf[at, :]
@@ -337,8 +367,8 @@
         newest = jnp.sum(asked * entries, axis=1, keepdims=True)
         raw = jnp.concatenate(
             [
-                dot_nt(asked[8 * u : 8 * u + 8].astype(BF), cache[n * group + u])
-                for u in range(group)
+                dot_nt(apart(asked[8 * u : 8 * u + 16]), both(n * group + u))
+                for u in range(0, group, 2)
             ],
             axis=0,
         )
@@ -351,17 +381,15 @@
         probs = (raised / total).astype(BF).astype(F32)
         newest_prob = (jnp.exp(newest - peak) / total).astype(BF).astype(F32)
         kept = jnp.where(current, 0.0, probs)
-        mixed = jnp.concatenate(
-            [
-                jnp.dot(
-                    kept[8 * u : 8 * u + 8].astype(BF),
-                    cache[n * group + u],
-                    preferred_element_type=F32,
-                )
-                for u in range(group)
-            ],
-            axis=0,
-        )
+        mixed = []
+        for u in range(0, group, 2):
+            pair = jnp.dot(
+                kept[8 * u : 8 * u + 16].astype(BF),
+                both(n * group + u),
+                preferred_element_type=F32,
+            )
+            mixed += [pair[:8, :LANES], pair[8:, LANES:]]
+        mixed = jnp.concatenate(mixed, axis=0)
         scb[at, :] = mixed + newest_prob * entries
         return c
 
@@ -462,6 +490,8 @@
             dispatch_copy(j, i).start()
         return c
 
+    lax.fori_loop(0, AHEAD, dispatch, 0)
+
     lifted = total * own_gain[...]
     wide_rows = jnp.zeros((LANES - TOK, PAD), BF)
     logit_part = jnp.zeros((experts, LANES), F32)
@@ -486,9 +516,6 @@
 
     for i in range(1, NTP):
         share(i).start()
-
-
-    lax.fori_loop(0, AHEAD, dispatch, 0)
 
     def scale_copy(j, i):
         zd = lax.rem(z + NZ - z_offset(j), NZ)
@@ -728,14 +755,13 @@
     expert_ids,
 ):
     vmem = pl.BlockSpec(memory_space=pltpu.VMEM)
-    smem = pl.BlockSpec(memory_space=pltpu.SMEM)
     hbm = pl.BlockSpec(memory_space=pl.ANY)
     dma = pltpu.SemaphoreType.DMA
     vm = pltpu.VMEM
     return pl.pallas_call(
         layer_body,
         out_shape=jax.ShapeDtypeStruct(tokens.shape, F32),
-        in_specs=[vmem, vmem, smem, vmem, vmem, vmem] + [hbm] * 6,
+        in_specs=[hbm] * 13,
         out_specs=vmem,
         scratch_shapes=[
             vm((NC, CHUNK, WIDE), BF),
@@ -752,6 +778,13 @@
             vm((TOK, LANES, 2 * HD), BF),
             vm((2 * PAD, FULL), BF),
             vm((PAD, FULL), BF),
+            vm((TOK, COL), BF),
+            vm((FULL,), F32),
+            vm((FULL,), F32),
+            pltpu.SMEM((HEADS,), F32),
+            vm((1, TOK), jnp.int32),
+            vm((NZ * NY, COL), BF),
+            vm((expert_ids.shape[1], TOK), jnp.int32),
             vm((1, WIDE), F32),
             vm((1, PAD), F32),
             vm((TOK, PAD), F32),
@@ -775,7 +808,7 @@
             vm((NZ * NY, PAD), BF),
             vm((NZ, 1, LANES), F32),
             vm((NZ * NY, 1, LANES), F32),
-            dma((28,)),
+            dma((35,)),
             dma((2,)),
             dma((NZ * NY,)),
             dma((NZ * NY,)),
@@ -796,7 +829,8 @@
         name="layer",
     )(
         tokens,
-        jnp.stack([attn_gain, moe_gain]),
+        attn_gain,
+        moe_gain,
         attn_sinks,
         positions[None, :],
         jnp.transpose(router),

time: 111 us -> 106 us (0.955)
  Pallas kernels: 107 us -> 104 us
  local copies, waits for them, and re-layouts: 3.01 us -> 1.58 us
    pallas_call x1, Pallas kernels: 107 us -> 104 us  [on_device(): pl.pallas_call(layer_body, out_shape=jax.ShapeDtypeStruct(tokens.shape, F...]
    another operation x2 -> x0, local copies, waits for them, and re-layouts: 1.43 us -> none  [on_device(): jnp.stack([attn_gain, moe_gain])]
where the time goes in v4:
time: 106 us
  Pallas kernels  104 us (98%)
  local copies, waits for them, and re-layouts  1.58 us (1%)
    pallas_call x1, Pallas kernels, on_device(): pl.pallas_call(layer_body, out_shape=jax.ShapeDtypeStruct(tokens.shape, F...  104 us

profile of v4, /device:TPU:1, one launch (start us, length us, event | category | flops | bytes accessed | tf_op | source)
XLA Modules:
  0.0 105.8 jit_solution(14221697935246670693)
XLA Ops:
  0.0 104.2 %layer.1 = f32[96,360]{1,0:T(8,128)} custom-call(bf16[96,360]{1,0:T(8,128)(2,1)} %tokens_hbm.1, f32[2880]{0:T(1024)} %again_hbm.1, f32[2880]{0:T(1024)} %mgain_hbm.1, f32[4]{0:T(128)} %sinks_hbm.1, s32[1,96]{1,0:T(1,128)} %bitcast.19, bf16[32,360]{1,0:T(8,128)(2,1)} %bitcast.17, s32[4,96]{1,0:T(4,128)} %bitcast.18, bf16[2880,256]{1,0:T(8,128)(2,1)} %wq_hbm.1, ...), custom_call_target="tpu_custom_call" | custom-call | tf_op jit(solution)/shard_map/layer/pallas_call | solution.py:761
  104.2 1.6 %copy.15 = f32[96,360]{1,0:T(8,128)} copy(f32[96,360]{1,0:T(8,128)} %layer.1) | data formatting | bytes 276480

commit v5 on v4

--- a/solution.py
+++ b/solution.py
@@ -36,7 +36,7 @@
 BF = jnp.bfloat16
 
 
-ORDER = (0, 1, 2, 4, 5, 3, 6, 7)
+ORDER = (0, 7, 2, 4, 3, 5, 6, 1)
 OWN = ORDER.index(0)
 SETTLE = 1
 AHEAD = 3
@@ -345,7 +345,7 @@
         sinks[0],
         jnp.where(sub == 1, sinks[1], jnp.where(sub == 2, sinks[2], sinks[3])),
     )[:, :1]
-    group = 48
+    group = 96
     sink = jnp.concatenate([sink] * group, axis=0)
     slots = lax.broadcasted_iota(jnp.int32, (8 * group, LANES), 1)
 

time: 106 us -> 105 us (level)
  no operation moved by 1% of the time
where the time goes in v5:
time: 105 us
  Pallas kernels  103 us (98%)
  local copies, waits for them, and re-layouts  1.58 us (2%)
    pallas_call x1, Pallas kernels, on_device(): pl.pallas_call(layer_body, out_shape=jax.ShapeDtypeStruct(tokens.shape, F...  103 us

profile of v5, /device:TPU:1, one launch (start us, length us, event | category | flops | bytes accessed | tf_op | source)
XLA Modules:
  0.0 104.8 jit_solution(16631746587426921682)
XLA Ops:
  0.0 103.2 %layer.1 = f32[96,360]{1,0:T(8,128)} custom-call(bf16[96,360]{1,0:T(8,128)(2,1)} %tokens_hbm.1, f32[2880]{0:T(1024)} %again_hbm.1, f32[2880]{0:T(1024)} %mgain_hbm.1, f32[4]{0:T(128)} %sinks_hbm.1, s32[1,96]{1,0:T(1,128)} %bitcast.19, bf16[32,360]{1,0:T(8,128)(2,1)} %bitcast.17, s32[4,96]{1,0:T(4,128)} %bitcast.18, bf16[2880,256]{1,0:T(8,128)(2,1)} %wq_hbm.1, ...), custom_call_target="tpu_custom_call" | custom-call | tf_op jit(solution)/shard_map/layer/pallas_call | solution.py:761
  103.2 1.6 %copy.15 = f32[96,360]{1,0:T(8,128)} copy(f32[96,360]{1,0:T(8,128)} %layer.1) | data formatting | bytes 276480
